TPU v7x, 16 devices: a whole 2x2x2 slice. The times are simulated.
16 devices in a mesh: sp: 16 (over z, y, x, core).
Axes of the slice: x: 2, y: 2, z: 2, core: 2. Of those that a mesh axis runs over, the one named last changes fastest.
Arguments:
- x_act: bfloat16 [4096, 1024], P('sp')
- positions: int32 [4096], P('sp')
- grad_out: bfloat16 [4096, 1024], P('sp')
- g_attn: bfloat16 [1024], P('sp')
- w_q: bfloat16 [1024, 16, 64], P('sp')
- w_k: bfloat16 [1024, 16, 64], P('sp')
- w_v: bfloat16 [1024, 16, 64], P('sp')
- w_o: bfloat16 [16, 64, 1024], P('sp')
- g_mlp: bfloat16 [1024], P('sp')
- w_gate: bfloat16 [1024, 2816], P('sp')
- w_up: bfloat16 [1024, 2816], P('sp')
- w_down: bfloat16 [2816, 1024], P('sp')
Outputs:
- output 1: bfloat16 [4096, 1024], P('sp')
- output 2: bfloat16 [4096, 1024], P('sp')
- output 3: float32 [1024], P('sp')
- output 4: float32 [1024, 16, 64], P('sp')
- output 5: float32 [1024, 16, 64], P('sp')
- output 6: float32 [1024, 16, 64], P('sp')
- output 7: float32 [16, 64, 1024], P('sp')
- output 8: float32 [1024], P('sp')
- output 9: float32 [1024, 2816], P('sp')
- output 10: float32 [1024, 2816], P('sp')
- output 11: float32 [2816, 1024], P('sp')
All inputs are finite; a program needn't handle non-finite values.
Results may differ from a plain program's by a relative error of at most 0.0169985.
Values are sent between devices in bfloat16 or wider.
A program may use at most 1 GiB of HBM per device.

v0:
```python
import jax
import jax.numpy as jnp
from jax import lax
from jax.experimental import pallas as pl
from jax.experimental.layout import Layout, with_layout_constraint
from jax.experimental.pallas import tpu as pltpu
from jax.sharding import PartitionSpec as P

SEQ_AXIS = 'sp'
RMS_EPS = 1e-5
ROPE_BASE = 10000.0
MASK_VALUE = -1e30
TILE = 512
F32 = jnp.float32
BF16 = jnp.bfloat16


def rms_norm(act_in, gain_vec):
    act_f = act_in.astype(F32)
    inv_rms = lax.rsqrt(jnp.mean(act_f * act_f, axis=-1, keepdims=True) + RMS_EPS)
    return (act_f * inv_rms * gain_vec.astype(F32)).astype(BF16), inv_rms


def rms_norm_bwd(act_in, gain_vec, inv_rms, d_normed):
    act_f = act_in.astype(F32)
    d_f = d_normed.astype(F32)
    scaled_d = d_f * gain_vec.astype(F32)
    proj_mean = jnp.mean(scaled_d * act_f, axis=-1, keepdims=True)
    d_act = inv_rms * scaled_d - act_f * (inv_rms * inv_rms * inv_rms) * proj_mean
    d_gain = jnp.sum(d_f * act_f * inv_rms, axis=0)
    return d_act, d_gain


def dot(lhs, rhs, l_dim, r_dim):
    return lax.dot_general(lhs, rhs, (((l_dim,), (r_dim,)), ((), ())), preferred_element_type=F32)


def gather(shard):
    return lax.all_gather(shard, SEQ_AXIS, axis=0, tiled=True)


def exchange(blocks):
    return lax.all_to_all(blocks, SEQ_AXIS, 0, 0, tiled=True)


def rope_t(vals, cos_tab, sin_tab):
    half = vals.shape[0] // 2
    first, second = vals[:half], vals[half:]
    return jnp.concatenate([first * cos_tab - second * sin_tab, second * cos_tab + first * sin_tab], axis=0)


def mm(lhs, rhs):
    return jnp.dot(lhs, rhs, preferred_element_type=F32)


def diag_mask(tile):
    key_at = lax.broadcasted_iota(jnp.int32, (tile, tile), 0)
    query_at = lax.broadcasted_iota(jnp.int32, (tile, tile), 1)
    return key_at <= query_at


def attn_fwd_kernel(tile, q_t, k_ref, v_t, o_ref, of_ref, lse_ref, s_buf):
    step = pl.program_id(0)
    query = q_t[...]

    def scores(j):
        return mm(k_ref[pl.ds(pl.multiple_of(j * tile, tile), tile), :], query)

    def keep(j, logits, top):
        s_buf[pl.ds(pl.multiple_of(j * tile, tile), tile), :] = logits
        return jnp.maximum(top, jnp.max(logits, axis=0, keepdims=True))

    top = keep(step, jnp.where(diag_mask(tile), scores(step), MASK_VALUE), jnp.full((1, tile), MASK_VALUE, F32))
    top = lax.fori_loop(0, step, lambda j, c: keep(j, scores(j), c), top)

    def weigh(j, carry):
        acc, total = carry
        at = pl.ds(pl.multiple_of(j * tile, tile), tile)
        prob = jnp.exp(s_buf[at, :] - top)
        return acc + mm(v_t[:, at], prob.astype(BF16)), total + jnp.sum(prob, axis=0, keepdims=True)

    out, total = lax.fori_loop(0, step + 1, weigh, (jnp.zeros((v_t.shape[0], tile), F32), jnp.zeros((1, tile), F32)))
    out = out / total
    lse = top + jnp.log(total)
    of_ref[...] = out
    lse_ref[...] = lse
    block = o_ref.shape[2]
    for part in range(tile // block):
        o_ref[part] = out[:, part * block:(part + 1) * block].astype(BF16)


def attention_fwd(q_t, k_in, v_t, n_blocks):
    head_dim, seq = q_t.shape
    block = seq // n_blocks
    per = TILE // block
    return pl.pallas_call(
        lambda *refs: attn_fwd_kernel(TILE, *refs),
        grid=(seq // TILE,),
        in_specs=[pl.BlockSpec((head_dim, TILE), lambda i: (0, i)), pl.BlockSpec((seq, head_dim), lambda i: (0, 0)), pl.BlockSpec((head_dim, seq), lambda i: (0, 0))],
        out_specs=[pl.BlockSpec((per, head_dim, block), lambda i: (i, 0, 0)), pl.BlockSpec((head_dim, TILE), lambda i: (0, i)), pl.BlockSpec((1, TILE), lambda i: (0, i))],
        out_shape=[jax.ShapeDtypeStruct((n_blocks, head_dim, block), BF16), jax.ShapeDtypeStruct((head_dim, seq), F32), jax.ShapeDtypeStruct((1, seq), F32)],
        scratch_shapes=[pltpu.VMEM((seq, TILE), F32)],
        cost_estimate=pl.CostEstimate(flops=8 * seq * seq * head_dim, bytes_accessed=8 * seq * head_dim, transcendentals=seq * seq),
        name='attn_fwd',
    )(q_t, k_in, v_t)


PARTS = ((0, 96), (96, 80), (176, 80))
CORE, CHIP_AXES = 1, (2, 4, 8)


def flip(dev, bit):
    return dev + bit * (1 - 2 * ((dev // bit) % 2))


def start_copy(src, dst, send_sem, recv_sem, peer):
    copy = pltpu.make_async_remote_copy(src_ref=src, dst_ref=dst, send_sem=send_sem, recv_sem=recv_sem, device_id=(peer,), device_id_type=pl.DeviceIdType.MESH)
    copy.start()
    return copy


def landed(ref, sem):
    pltpu.make_async_copy(ref, ref, sem).wait()


def enter_all(me, n_dev):
    barrier = pltpu.get_barrier_semaphore()

    @pl.loop(1, n_dev)
    def _(hop):
        pl.semaphore_signal(barrier, inc=1, device_id=(lax.rem(me + hop, n_dev),), device_id_type=pl.DeviceIdType.MESH)

    pl.semaphore_wait(barrier, n_dev - 1)


class CubeGather:
    def __init__(self, me, part, send_sem, recv_sem, core_sem):
        self.me, self.part = me, part
        self.send_sem, self.recv_sem, self.core_sem = send_sem, recv_sem, core_sem
        self.sent = []

    def axes(self, p):
        return [CHIP_AXES[(p + i) % 3] for i in range(3)]

    def owner(self, p, index, start=None):
        dev = self.me if start is None else start
        for i, bit in enumerate(self.axes(p)):
            if (index >> i) & 1:
                dev = flip(dev, bit)
        return dev

    def push(self, p, index, axis):
        ref = self.part(self.owner(p, index), p)
        start_copy(ref, ref, self.send_sem.at[len(self.sent)], self.recv_sem.at[p, index + (1 << axis)], flip(self.me, self.axes(p)[axis]))
        self.sent.append((p, index))

    def push_core(self, p, index):
        ref = self.part(self.owner(p, index), p)
        start_copy(ref, ref, self.send_sem.at[len(self.sent)], self.core_sem.at[p, index], flip(self.me, CORE))
        self.sent.append((p, index))

    def begin(self):
        for axis in range(3):
            for p in range(3):
                self.push(p, 0, axis)
        for p in range(3):
            self.push_core(p, 0)

    def receive(self, index):
        for p in range(3):
            landed(self.part(self.owner(p, index), p), self.recv_sem.at[p, index])
            for axis in range(index.bit_length(), 3):
                self.push(p, index, axis)
            self.push_core(p, index)

    def receive_core(self, index):
        for p in range(3):
            landed(self.part(self.owner(p, index, flip(self.me, CORE)), p), self.core_sem.at[p, index])

    def finish(self):
        for slot, (p, index) in enumerate(self.sent):
            landed(self.part(self.owner(p, index), p), self.send_sem.at[slot])


N_SENDS = 9 + 12 + 24


def attn_bwd_kernel(n_dev, tile, block, q_t, do_t, of_t, lse_ref, cos_ref, sin_ref, k_ref, k_t, v_ref, cos_all, sin_all, w_ref, d_blocks, d_proj_t, w_out_q, w_out_k, w_out_v, dq_acc, dk_acc, dv_acc, w_buf, send_sem, recv_sem, core_sem, local_sem):
    step = pl.program_id(0)
    last = pl.num_programs(0) - 1
    me = lax.axis_index(SEQ_AXIS)
    cube = CubeGather(me, lambda dev, p: w_buf.at[p, dev], send_sem, recv_sem, core_sem)

    @pl.when(step == 0)
    def _():
        own = [pltpu.make_async_copy(w_ref.at[p], w_buf.at[p, me], local_sem.at[p]) for p in range(3)]
        for copy in own:
            copy.start()
        enter_all(me, n_dev)
        for copy in own:
            copy.wait()
        cube.begin()

    for at_step, indices in ((4, (1,)), (5, (2,)), (6, (4,)), (7, (3,))):
        @pl.when(step == at_step)
        def _(indices=indices):
            for index in indices:
                cube.receive(index)

    head_dim = q_t.shape[0]
    query_t, d_out_t = q_t[...], do_t[...]
    lse = lse_ref[...]
    delta = jnp.sum(d_out_t.astype(F32) * of_t[...], axis=0, keepdims=True)

    @pl.when(step == 0)
    def _():
        dk_acc[...] = jnp.zeros_like(dk_acc)
        dv_acc[...] = jnp.zeros_like(dv_acc)

    dq_acc[...] = jnp.zeros_like(dq_acc)

    def visit(j, masked):
        at = pl.ds(pl.multiple_of(j * tile, tile), tile)
        prob = jnp.exp(mm(k_ref[at, :], query_t) - lse)
        if masked:
            prob = jnp.where(diag_mask(tile), prob, 0.0)
        d_prob = mm(v_ref[at, :], d_out_t).astype(BF16).astype(F32)
        d_logits = (prob * (d_prob - delta)).astype(BF16)
        dv_acc[:, at] += dot(d_out_t, prob.astype(BF16), 1, 1)
        dk_acc[:, at] += dot(query_t, d_logits, 1, 1)
        dq_acc[...] += mm(k_t[:, at], d_logits)

    visit(step, True)

    @pl.loop(0, step)
    def _(j):
        visit(j, False)

    def put(row, col_block, values):
        rows = slice(row, row + values.shape[0])
        d_proj_t[rows, pl.ds(pl.multiple_of(col_block * block, block), values.shape[1])] = values
        for part in range(values.shape[1] // block):
            d_blocks[col_block + part, rows, :] = values[:, part * block:(part + 1) * block]

    d_q = (dq_acc[...] * (head_dim ** -0.5)).astype(BF16).astype(F32)
    per = tile // block
    put(0, step * per, rope_t(d_q, cos_ref[...], -sin_ref[...]).astype(BF16))

    @pl.when(step == last)
    def _():
        @pl.loop(0, pl.num_programs(0))
        def _(j):
            at = pl.ds(pl.multiple_of(j * tile, tile), tile)
            put(head_dim, j * per, rope_t(dk_acc[:, at].astype(BF16).astype(F32), cos_all[:, at], -sin_all[:, at]).astype(BF16))
            put(2 * head_dim, j * per, dv_acc[:, at].astype(BF16))

        for index in (5, 6, 7):
            cube.receive(index)
        for index in range(8):
            cube.receive_core(index)
        flushes = [pltpu.make_async_copy(w_buf.at[p], out, local_sem.at[p]) for p, out in enumerate((w_out_q, w_out_k, w_out_v))]
        for flush in flushes:
            flush.start()
        cube.finish()
        for flush in flushes:
            flush.wait()


def attention_bwd(q_t, do_t, of_t, lse, k_in, k_t, v_in, cos_t, sin_t, w_parts, n_blocks):
    head_dim, seq = q_t.shape
    block = seq // n_blocks
    cols = pl.BlockSpec((head_dim, TILE), lambda i: (0, i))
    half_cols = pl.BlockSpec((head_dim // 2, TILE), lambda i: (0, i))
    all_rows = pl.BlockSpec((seq, head_dim), lambda i: (0, 0))
    all_cols = pl.BlockSpec((head_dim, seq), lambda i: (0, 0))
    all_half = pl.BlockSpec((head_dim // 2, seq), lambda i: (0, 0))
    w_all_shape = (3, n_blocks) + w_parts.shape[1:]
    return pl.pallas_call(
        lambda *refs: attn_bwd_kernel(n_blocks, TILE, block, *refs),
        grid=(seq // TILE,),
        in_specs=[cols, cols, cols, pl.BlockSpec((1, TILE), lambda i: (0, i)), half_cols, half_cols, all_rows, all_cols, all_rows, all_half, all_half, pl.BlockSpec(memory_space=pl.ANY)],
        out_specs=[pl.BlockSpec((n_blocks, 3 * head_dim, block), lambda i: (0, 0, 0)), pl.BlockSpec((3 * head_dim, seq), lambda i: (0, 0))] + [pl.BlockSpec(memory_space=pl.ANY)] * 3,
        out_shape=[jax.ShapeDtypeStruct((n_blocks, 3 * head_dim, block), BF16), jax.ShapeDtypeStruct((3 * head_dim, seq), BF16)] + [jax.ShapeDtypeStruct(w_all_shape[1:], BF16)] * 3,
        scratch_shapes=[
            pltpu.VMEM((head_dim, TILE), F32),
            pltpu.VMEM((head_dim, seq), F32),
            pltpu.VMEM((head_dim, seq), F32),
            pltpu.VMEM(w_all_shape, BF16),
            pltpu.SemaphoreType.DMA((N_SENDS,)),
            pltpu.SemaphoreType.DMA((3, 8)),
            pltpu.SemaphoreType.DMA((3, 8)),
            pltpu.SemaphoreType.DMA((3,)),
        ],
        compiler_params=pltpu.CompilerParams(collective_id=1, has_side_effects=True),
        cost_estimate=pl.CostEstimate(flops=20 * seq * seq * head_dim, bytes_accessed=20 * seq * head_dim, transcendentals=seq * seq),
        name='attn_bwd',
    )(q_t, do_t, of_t, lse, cos_t, sin_t, k_in, k_t, v_in, cos_t, sin_t, w_parts)


def gather_proj_kernel(n_dev, x_ref, small_ref, w_ref, u_out, proj_t, small_all, x_buf, u_buf, w_buf, send_sem, recv_sem, core_sem, misc_send, misc_recv, local_sem, u_sem):
    me = lax.axis_index(SEQ_AXIS)
    own = pltpu.make_async_copy(x_ref, x_buf.at[me], local_sem.at[0])
    own.start()
    own_w = pltpu.make_async_copy(w_ref.at[me], w_buf.at[me], local_sem.at[1])
    own_w.start()
    own_small = pltpu.make_async_copy(small_ref, small_all.at[me], local_sem.at[2])
    own_small.start()
    enter_all(me, n_dev)
    own.wait()
    cube = CubeGather(me, lambda dev, p: x_buf.at[dev, pl.ds(PARTS[p][0], PARTS[p][1])], send_sem, recv_sem, core_sem)
    cube.begin()

    def spread(hop):
        peer = lax.rem(me + hop, n_dev)
        return [
            pltpu.make_async_remote_copy(src_ref=small_ref, dst_ref=small_all.at[me], send_sem=misc_send.at[0, hop], recv_sem=misc_recv.at[0, me], device_id=(peer,), device_id_type=pl.DeviceIdType.MESH),
            pltpu.make_async_remote_copy(src_ref=w_ref.at[peer], dst_ref=w_buf.at[me], send_sem=misc_send.at[1, hop], recv_sem=misc_recv.at[1, me], device_id=(peer,), device_id_type=pl.DeviceIdType.MESH),
        ]

    for kind in range(2):
        @pl.loop(1, n_dev)
        def _(hop, kind=kind):
            spread(hop)[kind].start()

    cube.receive(1)
    cube.receive(2)
    own_w.wait()
    own_small.wait()

    @pl.loop(1, n_dev)
    def _(hop):
        src = lax.rem(me + hop, n_dev)
        landed(small_all.at[src], misc_recv.at[0, src])
        landed(w_buf.at[src], misc_recv.at[1, src])

    width = x_ref.shape[1]
    tok = x_ref.shape[0]
    rows = w_ref.shape[1]
    gain = jnp.concatenate([small_all[d, 0:1, 0:rows] for d in range(n_dev)], axis=1)
    weight = w_buf[...].reshape(width, w_ref.shape[2])
    keep = proj_t.shape[0]

    def project(dev):
        act = x_buf[dev].astype(F32)
        inv = lax.rsqrt(jnp.mean(act * act, axis=-1, keepdims=True) + RMS_EPS)
        normed = (act * inv * gain).astype(BF16)
        u_buf[dev] = normed
        proj_t[:, pl.ds(pl.multiple_of(dev * tok, tok), tok)] = mm(normed, weight).T[:keep]
        pltpu.make_async_copy(u_buf.at[dev], u_out.at[dev], u_sem.at[dev]).start()

    def project_pair(dev):
        @pl.loop(0, 2)
        def _(core):
            project(dev + core * (flip(dev, CORE) - dev))

    def project_across(dev):
        @pl.loop(0, 3)
        def _(i):
            project_pair(flip(dev, i * (i + 1) + 2))

    cube.receive_core(0)
    project_pair(me)
    cube.receive(4)
    cube.receive(3)
    for index in (1, 2, 4):
        cube.receive_core(index)
    project_across(me)
    cube.receive(5)
    cube.receive(6)
    for index in (3, 5, 6):
        cube.receive_core(index)
    far = flip(flip(flip(me, 2), 4), 8)
    project_across(far)
    cube.receive(7)
    cube.receive_core(7)
    project_pair(far)

    cube.finish()

    @pl.loop(1, n_dev)
    def _(hop):
        for copy in spread(hop):
            copy.wait_send()

    @pl.loop(0, n_dev)
    def _(dev):
        pltpu.make_async_copy(u_buf.at[dev], u_out.at[dev], u_sem.at[dev]).wait()


def gather_proj(n_dev, x_act, small, w_blocks, qkv):
    tok, width = x_act.shape
    seq = tok * n_dev
    any_spec = pl.BlockSpec(memory_space=pl.ANY)
    vmem_spec = pl.BlockSpec(memory_space=pltpu.VMEM)
    return pl.pallas_call(
        lambda *refs: gather_proj_kernel(n_dev, *refs),
        in_specs=[any_spec, vmem_spec, vmem_spec],
        out_specs=[any_spec, vmem_spec, vmem_spec],
        out_shape=[jax.ShapeDtypeStruct((n_dev, tok, width), BF16), jax.ShapeDtypeStruct((qkv, seq), F32), jax.ShapeDtypeStruct((n_dev,) + small.shape, F32)],
        scratch_shapes=[
            pltpu.VMEM((n_dev, tok, width), BF16),
            pltpu.VMEM((n_dev, tok, width), BF16),
            pltpu.VMEM(w_blocks.shape, BF16),
            pltpu.SemaphoreType.DMA((N_SENDS,)),
            pltpu.SemaphoreType.DMA((3, 8)),
            pltpu.SemaphoreType.DMA((3, 8)),
            pltpu.SemaphoreType.DMA((2, n_dev)),
            pltpu.SemaphoreType.DMA((2, n_dev)),
            pltpu.SemaphoreType.DMA((3,)),
            pltpu.SemaphoreType.DMA((n_dev,)),
        ],
        compiler_params=pltpu.CompilerParams(collective_id=0, has_side_effects=True),
        cost_estimate=pl.CostEstimate(flops=30 * seq * width * width, bytes_accessed=4 * seq * width, transcendentals=0),
        name='gather_proj',
    )(x_act, small, w_blocks)


def gate_backward(d_mixed, gate_pre, up_pre):
    gate_sig = jax.nn.sigmoid(gate_pre)
    d_up = (d_mixed * gate_pre * gate_sig).astype(BF16)
    d_gate = (d_mixed * up_pre * gate_sig * (1.0 + gate_pre * (1.0 - gate_sig))).astype(BF16)
    return d_gate, d_up


def join_columns_kernel(size, src, first, second):
    turned = [src[d, :size, :].T for d in range(src.shape[0])]
    rows = first.shape[0]
    first[...] = jnp.concatenate([block[:rows] for block in turned], axis=1)
    second[...] = jnp.concatenate([block[rows:] for block in turned], axis=1)


def join_columns(blocks, size):
    shape = jax.ShapeDtypeStruct((blocks.shape[2] // 2, blocks.shape[0] * size), F32)
    return pl.pallas_call(lambda *refs: join_columns_kernel(size, *refs), out_shape=[shape, shape], name='join_columns')(blocks)


def split_heads_kernel(head_dim, src, first, second, third):
    half = head_dim // 2
    for d in range(src.shape[0]):
        turned = src[d].T
        low, high = turned[:head_dim], turned[head_dim:]
        first[:, d, :] = low[:, :head_dim]
        second[:, d, :] = jnp.concatenate([low[:, head_dim:], high[:, :half]], axis=1)
        third[:, d, :] = high[:, half:]


def split_heads(blocks, head_dim):
    shape = jax.ShapeDtypeStruct((blocks.shape[2] // 2, blocks.shape[0], head_dim), F32)
    return pl.pallas_call(lambda *refs: split_heads_kernel(head_dim, *refs), out_shape=[shape] * 3, name='split_heads')(blocks)


def pack_pairs_kernel(rows, grad_t, *refs):
    out = refs[-1]
    half = grad_t.shape[0] // 2
    for d in range(out.shape[0]):
        at = slice(d * rows, (d + 1) * rows)
        out[d, :half, :] = jnp.concatenate([grad_t[:half, at], grad_t[half:, at]], axis=1)
        if len(refs) > 1:
            out[d, half:, :] = refs[0][d]


def pack_pairs(grad_t, n_dev, rows, *tail):
    height = grad_t.shape[0] // 2 + sum(part.shape[1] for part in tail)
    shape = jax.ShapeDtypeStruct((n_dev, height, 2 * rows), F32)
    return pl.pallas_call(lambda *refs: pack_pairs_kernel(rows, *refs), out_shape=shape, name='pack_pairs')(grad_t, *tail)


def weight_block_kernel(gate, up, w_o, down, out):
    rows = gate.shape[0]
    at = 0
    for part in (gate[...], up[...], w_o[0]):
        out[:, at:at + part.shape[1]] = part
        at += part.shape[1]
    for start in range(0, down.shape[0], rows):
        height = min(rows, down.shape[0] - start)
        out[:height, at:at + down.shape[1]] = down[start:start + height, :]
        if height < rows:
            out[height:, at:at + down.shape[1]] = jnp.zeros((rows - height, down.shape[1]), BF16)
        at += down.shape[1]


def weight_block(gate, up, w_o, down):
    rows = gate.shape[0]
    width = 2 * gate.shape[1] + w_o.shape[2] + pl.cdiv(down.shape[0], rows) * down.shape[1]
    return pl.pallas_call(weight_block_kernel, out_shape=jax.ShapeDtypeStruct((rows, width), BF16), name='weight_block')(gate, up, w_o, down)


def device_step(n_dev, x_act, positions, grad_out, g_attn_s, w_q, w_k, w_v, w_o, g_mlp_s, w_gate, w_up, w_down):
    tok, width = x_act.shape
    seq = tok * n_dev
    rows, heads, head_dim = w_q.shape
    ff = w_gate.shape[1]
    ff_s = ff // n_dev
    qkv = 3 * head_dim

    small = jnp.concatenate([jnp.concatenate([g_attn_s, g_mlp_s]).astype(F32)[None], positions.astype(F32).reshape(-1, 2 * rows)], axis=0)
    small = jnp.pad(small, ((0, 8 - small.shape[0]), (0, 0)))
    w_qkv = jnp.concatenate([w_q, w_k, w_v], axis=2)
    w_blocks = jnp.pad(jnp.transpose(w_qkv, (1, 0, 2)), ((0, 0), (0, 0), (0, 256 - qkv)))
    u_all, proj_t, small_all = gather_proj(n_dev, x_act, small, w_blocks, qkv)
    u_all = u_all.reshape(seq, width)
    g_attn = small_all[:, 0, :rows].reshape(width)
    g_mlp = small_all[:, 0, rows:2 * rows].reshape(width)
    pos_all = small_all[:, 1:1 + tok // (2 * rows)]

    w_all = gather(weight_block(w_gate, w_up, w_o, w_down))
    w_gu = w_all[:, :2 * ff]
    w_o_all = w_all[:, 2 * ff:2 * ff + width]
    w_down_at = 2 * ff + width
    down_all = [w_all[:, w_down_at + i * width:w_down_at + (i + 1) * width].reshape(n_dev, rows, width) for i in range(pl.cdiv(ff_s, rows))]
    w_down_all = jnp.concatenate(down_all, axis=1)[:, :ff_s].reshape(ff, width)
    me = lax.axis_index(SEQ_AXIS)
    w_cols = jnp.concatenate([lax.dynamic_slice(w_all, (0, at + me * ff_s), (width, ff_s)) for at in (0, ff)], axis=1)

    half = head_dim // 2
    inv_freq = ROPE_BASE ** (-(jnp.arange(half, dtype=F32) * (2.0 / head_dim)))
    angle_t = inv_freq[:, None] * pos_all.reshape(1, seq)
    cos_t, sin_t = jnp.cos(angle_t), jnp.sin(angle_t)

    q_t = (rope_t(proj_t[:head_dim], cos_t, sin_t).astype(BF16).astype(F32) * (head_dim ** -0.5)).astype(BF16)
    k_t = rope_t(proj_t[head_dim:2 * head_dim], cos_t, sin_t).astype(BF16)
    v_t = proj_t[2 * head_dim:].astype(BF16)
    k_in, v_in = k_t.T, v_t.T
    o_blocks, of_t, lse = attention_fwd(q_t, k_in, v_t, n_dev)
    o_loc = exchange(o_blocks).reshape(width, tok)
    w_parts = jnp.stack([w.reshape(rows, heads * head_dim) for w in (w_q, w_k, w_v)])
    o_loc, w_parts, v_in, w_down_all = lax.optimization_barrier((o_loc, w_parts, v_in, w_down_all))

    hidden = (x_act.astype(F32) + dot(o_loc, w_o_all, 0, 0)).astype(BF16)
    normed_mlp, inv_rms_mlp = rms_norm(hidden, g_mlp)
    a_dy = jnp.concatenate([normed_mlp, grad_out], axis=1)
    normed_mlp, a_dy = lax.optimization_barrier((normed_mlp, a_dy))
    a_dy = gather(a_dy)
    pre = with_layout_constraint(dot(normed_mlp, w_gu, 1, 0), Layout(major_to_minor=(0, 1)))
    gate_pre, up_pre = pre[:, :ff], pre[:, ff:]
    mixed = (jax.nn.silu(gate_pre) * up_pre).astype(BF16)
    y_out = (hidden.astype(F32) + dot(mixed, w_down_all, 1, 0)).astype(BF16)

    d_mixed = dot(grad_out, w_down_all, 1, 1).astype(BF16).astype(F32)
    d_gu = jnp.concatenate(gate_backward(d_mixed, gate_pre, up_pre), axis=1)
    d_normed = dot(d_gu, w_gu, 1, 1).astype(BF16)
    d_hid_norm, part_g_mlp = rms_norm_bwd(hidden, g_mlp, inv_rms_mlp, d_normed)
    d_hidden = (grad_out.astype(F32) + d_hid_norm).astype(BF16)
    do_blocks = exchange(dot(w_o_all, d_hidden, 1, 1).astype(BF16).reshape(n_dev, head_dim, tok))
    half_n = n_dev // 2
    pairs = [(i, (i + half_n) % n_dev) for i in range(n_dev)]
    near = (me // half_n) * half_n
    o_far = lax.ppermute(lax.dynamic_slice_in_dim(o_blocks, half_n - near, half_n), SEQ_AXIS, pairs)
    do_blocks, y_out = lax.optimization_barrier((do_blocks, y_out))
    dh_half = lax.all_gather(d_hidden, SEQ_AXIS, axis=0, tiled=True, axis_index_groups=[list(range(half_n)), list(range(half_n, n_dev))])

    do_t = jnp.transpose(do_blocks, (1, 0, 2)).reshape(head_dim, seq)
    d_blocks, d_proj_t, *w_qkv_all = attention_bwd(q_t, do_t, of_t, lse, k_in, k_t, v_in, cos_t, sin_t, w_parts, n_dev)
    d_proj = exchange(d_blocks)

    attn_send = pack_pairs(dot(d_proj_t, u_all, 1, 0), n_dev, rows)
    d_proj, attn_send = lax.optimization_barrier((d_proj, attn_send))
    attn_back = exchange(attn_send)
    d_proj = d_proj.reshape(heads, 3, head_dim, tok)
    inv_rms = lax.rsqrt(jnp.mean(jnp.square(x_act.astype(F32)), axis=-1, keepdims=True) + RMS_EPS)
    d_u = sum(dot(d_proj[:, p].reshape(heads * head_dim, tok), w_qkv_all[p].reshape(width, heads * head_dim), 0, 1) for p in range(3)).astype(BF16)
    d_x_norm, part_g_attn = rms_norm_bwd(x_act, g_attn, inv_rms, d_u)
    grad_x = (d_hidden.astype(F32) + d_x_norm).astype(BF16)
    gain_send = jnp.concatenate([part_g_attn.reshape(n_dev, 1, rows), part_g_mlp.reshape(n_dev, 1, rows)], axis=2)

    a_all, dy_all = a_dy[:, :width], a_dy[:, width:]
    pre_t = dot(w_cols, a_all, 0, 1)
    gate_t, up_t = pre_t[:ff_s], pre_t[ff_s:]
    d_mixed_t = dot(w_down, dy_all, 1, 1).astype(BF16).astype(F32)
    mixed_t = (jax.nn.silu(gate_t) * up_t).astype(BF16)
    d_gu_t = jnp.concatenate(gate_backward(d_mixed_t, gate_t, up_t), axis=0)
    mlp_send = pack_pairs(dot(d_gu_t, a_all, 1, 0), n_dev, rows, jnp.pad(gain_send, ((0, 0), (0, 7), (0, 0))))
    attn_back, mlp_send, mixed_t = lax.optimization_barrier((attn_back, mlp_send, mixed_t))
    mlp_back = exchange(mlp_send)
    grad_w_down = dot(mixed_t, dy_all, 1, 0)

    o_far, dh_half, o_blocks, grad_w_down = lax.optimization_barrier((o_far, dh_half, o_blocks, grad_w_down))
    o_pair = jnp.concatenate([lax.dynamic_slice_in_dim(o_blocks, near, half_n), o_far], axis=1)
    part_w_o = dot(o_pair.transpose(1, 0, 2).reshape(2 * head_dim, seq // 2), dh_half, 1, 0)
    grad_w_o = (part_w_o[:head_dim] + lax.ppermute(part_w_o[head_dim:], SEQ_AXIS, pairs))[None]

    grad_w_q, grad_w_k, grad_w_v = split_heads(attn_back, head_dim)
    mlp_back, grad_w_down, grad_w_q, grad_w_k, grad_w_v, grad_w_o = lax.optimization_barrier((mlp_back, grad_w_down, grad_w_q, grad_w_k, grad_w_v, grad_w_o))
    gains = jnp.sum(mlp_back[:, ff_s], axis=0)
    grad_g_attn, grad_g_mlp = gains[:rows], gains[rows:]
    grad_w_gate, grad_w_up = join_columns(mlp_back, ff_s)
    return (y_out, grad_x, grad_g_attn, grad_w_q, grad_w_k, grad_w_v, grad_w_o, grad_g_mlp, grad_w_gate, grad_w_up, grad_w_down)


def solution(mesh):
    n_dev = mesh.shape[SEQ_AXIS]
    token_spec = P(SEQ_AXIS, None)
    cube_spec = P(SEQ_AXIS, None, None)
    gain_spec = P(SEQ_AXIS)
    weight_specs = (gain_spec, cube_spec, cube_spec, cube_spec, cube_spec, gain_spec, token_spec, token_spec, token_spec)
    return jax.shard_map(lambda *args: device_step(n_dev, *args), mesh=mesh, in_specs=(token_spec, gain_spec, token_spec) + weight_specs, out_specs=(token_spec, token_spec) + weight_specs, check_vma=False)
```

profile of v0, /device:TPU:0, one launch (start us, length us, event | category | flops | bytes accessed | tf_op | source)
XLA Modules:
  0.0 326.7 jit_solution(11074867505769132570)
XLA Ops:
  11.8 67.8 %gather_proj.1 = (bf16[16,256,1024]{2,1,0:T(8,128)(2,1)}, f32[192,4096]{1,0:T(8,128)}, f32[16,8,128]{2,1,0:T(8,128)}) custom-call(bf16[256,1024]{1,0:T(8,128)(2,1)} %refs_0_.1, f32[8,128]{1,0:T(8,128)} %select_maximum_fusion.1.refs_1_, bf16[16,64,256]{2,1,0:T(8,128)(2,1)} %pad.13.refs_2_), custom_call_target="tpu_custom_call" | custom-call | flops 128849018880 | bytes 16777216 | tf_op jit(solution)/shard_map/gather_proj/pallas_call | solution.py:395
  82.6 5.3 %fusion.85 = (bf16[32,4096]{1,0:T(8,128)(2,1)S(1)}, bf16[32,4096]{1,0:T(8,128)(2,1)S(1)}, bf16[32,4096]{1,0:T(8,128)(2,1)S(1)}, bf16[32,4096]{1,0:T(8,128)(2,1)S(1)}, f32[32,4096]{1,0:T(8,128)}, /*index=5*/f32[32,4096]{1,0:T(8,128)}) fusion(f32[192,4096]{1,0:T(8,128)} %get-tuple-element.50, f32[4096]{0:T(1024)S(1)} %bitcast.72, f32[32]{0:T(128)S(1)} %negate_power_fusion), kind=kLoop, calls=%fused_computation.100 | loop fusion | flops 2228224 | bytes 4210816 | tf_op jit(solution)/shard_map/convert.3
  91.0 23.6 %attn_fwd.1 = (bf16[16,64,256]{2,1,0:T(8,128)(2,1)}, f32[64,4096]{1,0:T(8,128)}, f32[1,4096]{1,0:T(1,128)}) custom-call(bf16[64,4096]{1,0:T(8,128)(2,1)} %multiply_convert_fusion.11.refs_0_, bf16[4096,64]{1,0:T(8,128)(2,1)} %copy.56.refs_1_.refs_6_, bf16[64,4096]{1,0:T(8,128)(2,1)} %slice.201.refs_2_), custom_call_target="tpu_custom_call" | custom-call | flops 8589934592 | bytes 2097152 | tf_op jit(solution)/shard_map/attn_fwd/pallas_call | solution.py:96
  114.5 4.1 %all-to-all-start = ((bf16[16,64,256]{2,1,0:T(8,128)(2,1)}), bf16[16,64,256]{2,1,0:T(8,128)(2,1)S(1)}, u32[]{:S(2)}, u32[]{:S(2)}) async-start(bf16[16,64,256]{2,1,0:T(8,128)(2,1)} %get-tuple-element.78), calls=%async_computation | async-start | bytes 1048576 | tf_op jit(solution)/shard_map/all_to_all | solution.py:43
  123.4 3.6 %fusion.94 = (bf16[1024,1024]{1,0:T(8,128)(2,1)S(1)}, bf16[1024,1024]{1,0:T(8,128)(2,1)S(1)}, bf16[1024,1024]{1,0:T(8,128)(2,1)S(1)}) fusion(bf16[1024,9728]{1,0:T(8,128)(2,1)} %all-gather.4.cloned.1.call-done), kind=kLoop, calls=%fused_computation.134 | loop fusion | bytes 12582912 | tf_op jit(solution)/shard_map/slice | solution.py:510
  127.0 3.2 pad_maximum_fusion
  135.7 6.3 %fusion.2 = f32[256,5632]{1,0:T(8,128)S(1)} fusion(bf16[256,1024]{1,0:T(8,128)(2,1)} %copy-done.10, bf16[1024,9728]{1,0:T(8,128)(2,1)} %all-gather.4.cloned.1.call-done), kind=kOutput, calls=%fused_computation.2 | convolution fusion | flops 2952790016 | bytes 17825792 | tf_op jit(solution)/shard_map/dot_general | solution.py:35
  144.7 7.6 %fusion.68 = (f32[1024]{0:T(1024)S(1)}, f32[256]{0:T(256)S(1)}, bf16[256,1024]{1,0:T(8,128)(2,1)S(1)}) fusion(bf16[256,1024]{1,0:T(8,128)(2,1)S(1)} %get-tuple-element.123, f32[256]{0:T(256)S(1)} %get-tuple-element.119, f32[1024]{0:T(1024)S(1)} %mul.270, bf16[1024,9728]{1,0:T(8,128)(2,1)} %all-gather.4.cloned.1.call-done, ...), kind=kOutput, calls=%fused_computation.78 | convolution fusion | flops 2960915200 | bytes 15476736 | tf_op jit(solution)/shard_map/dot_general | solution.py:35
  152.7 3.3 %fusion.45 = bf16[1024,256]{1,0:T(8,128)(2,1)} fusion(bf16[256,1024]{1,0:T(8,128)(2,1)S(1)} %fusion.56, bf16[1024,9728]{1,0:T(8,128)(2,1)} %all-gather.4.cloned.1.call-done), kind=kOutput, calls=%fused_computation.57 | convolution fusion | flops 537133056 | bytes 3145728 | tf_op jit(solution)/shard_map/dot_general | solution.py:35
  156.0 3.4 %all-to-all-start.1 = ((bf16[16,64,256]{2,1,0:T(8,128)(2,1)}), bf16[16,64,256]{2,1,0:T(8,128)(2,1)S(1)}, u32[]{:S(2)}, u32[]{:S(2)}) async-start(bf16[16,64,256]{2,1,0:T(8,128)(2,1)} %bitcast.13), calls=%async_computation.1 | async-start | bytes 1048576 | tf_op jit(solution)/shard_map/all_to_all | solution.py:43
  160.2 6.9 %fusion.39 = bf16[256,1024]{1,0:T(8,128)(2,1)} fusion(bf16[2816,1024]{1,0:T(8,128)(2,1)} %bitcast.58, f32[256,5632]{1,0:T(8,128)} %copy-done.24, bf16[256,1024]{1,0:T(8,128)(2,1)S(1)} %get-tuple-element.123), kind=kOutput, calls=%fused_computation.55 | convolution fusion | flops 1481506816 | bytes 12582912 | tf_op jit(solution)/shard_map/dot_general | solution.py:35
  167.1 8.9 %all-to-all-done.1 = bf16[16,64,256]{2,1,0:T(8,128)(2,1)S(1)} async-done(((bf16[16,64,256]{2,1,0:T(8,128)(2,1)}), bf16[16,64,256]{2,1,0:T(8,128)(2,1)S(1)}, u32[]{:S(2)}, u32[]{:S(2)}) %all-to-all-start.1) | async-done | bytes 524320 | tf_op jit(solution)/shard_map/all_to_all | solution.py:43
  176.9 46.5 %attn_bwd.1 = (bf16[16,192,256]{2,1,0:T(8,128)(2,1)}, bf16[192,4096]{1,0:T(8,128)(2,1)}, bf16[16,64,1024]{2,1,0:T(8,128)(2,1)}, bf16[16,64,1024]{2,1,0:T(8,128)(2,1)}, bf16[16,64,1024]{2,1,0:T(8,128)(2,1)}) custom-call(bf16[64,4096]{1,0:T(8,128)(2,1)} %multiply_convert_fusion.11.refs_0_, bf16[64,4096]{1,0:T(8,128)(2,1)} %bitcast.70, ...), custom_call_target="tpu_custom_call" | custom-call | flops 21474836480 | bytes 5242880 | tf_op jit(solution)/shard_map/attn_bwd/pallas_call | solution.py:278
  223.3 3.7 %all-to-all-start.2 = ((bf16[16,192,256]{2,1,0:T(8,128)(2,1)}), bf16[16,192,256]{2,1,0:T(8,128)(2,1)S(1)}, u32[]{:S(2)}, u32[]{:S(2)}) async-start(bf16[16,192,256]{2,1,0:T(8,128)(2,1)} %get-tuple-element.62), calls=%async_computation.2 | async-start | bytes 3145728 | tf_op jit(solution)/shard_map/all_to_all | solution.py:43
  232.9 6.6 %fusion.97.refs_0_ = f32[192,1024]{1,0:T(8,128)} fusion(bf16[192,4096]{1,0:T(8,128)(2,1)} %get-tuple-element.63, bf16[4096,1024]{1,0:T(8,128)(2,1)} %bitcast.75), kind=kOutput, calls=%fused_computation.137 | convolution fusion | flops 1610612736 | bytes 10747904 | tf_op jit(solution)/shard_map/dot_general | solution.py:35
  241.8 8.9 %all-to-all-done.2 = bf16[16,192,256]{2,1,0:T(8,128)(2,1)S(1)} async-done(((bf16[16,192,256]{2,1,0:T(8,128)(2,1)}), bf16[16,192,256]{2,1,0:T(8,128)(2,1)S(1)}, u32[]{:S(2)}, u32[]{:S(2)}) %all-to-all-start.2) | async-done | bytes 1572896 | tf_op jit(solution)/shard_map/all_to_all | solution.py:43
  259.7 10.5 %fusion.6 = f32[352,4096]{1,0:T(8,128)} fusion(bf16[4096,2048]{1,0:T(8,128)(2,1)} %all-gather.6.cloned.1.call-done, bf16[1024,176]{1,0:T(8,128)(2,1)S(1)} %copy-done.17, bf16[1024,176]{1,0:T(8,128)(2,1)S(1)} %copy-done.16), kind=kOutput, calls=%fused_computation.6 | convolution fusion | flops 2954231808 | bytes 14876672 | tf_op jit(solution)/shard_map/dot_general | solution.py:35
  270.2 6.8 %multiply_convert_fusion.2 = (bf16[176,4096]{1,0:T(8,128)(2,1)S(1)}, bf16[176,4096]{1,0:T(8,128)(2,1)S(1)}, bf16[176,4096]{1,0:T(8,128)(2,1)}) fusion(f32[352,4096]{1,0:T(8,128)} %fusion.6, bf16[176,1024]{1,0:T(8,128)(2,1)S(1)} %copy-done.18, bf16[4096,2048]{1,0:T(8,128)(2,1)S(1)} %copy-done.20), kind=kOutput, calls=%fused_computation.28 | convolution fusion | flops 1489371136 | bytes 18841600 | tf_op jit(solution)/shard_map/dot_general | solution.py:35
  277.0 4.3 %fusion.4.refs_0_ = f32[352,1024]{1,0:T(8,128)} fusion(bf16[4096,2048]{1,0:T(8,128)(2,1)S(1)} %copy-done.20, bf16[176,4096]{1,0:T(8,128)(2,1)S(1)} %get-tuple-element.101, bf16[176,4096]{1,0:T(8,128)(2,1)S(1)} %get-tuple-element.100), kind=kOutput, calls=%fused_computation.4 | convolution fusion | flops 2958557184 | bytes 12713984 | tf_op jit(solution)/shard_map/dot_general | solution.py:35
  284.3 4.1 %all-to-all-start.4 = ((f32[16,184,128]{2,1,0:T(8,128)}), f32[16,184,128]{2,1,0:T(8,128)S(1)}, u32[]{:S(2)}, u32[]{:S(2)}) async-start(f32[16,184,128]{2,1,0:T(8,128)} %pack_pairs.3), calls=%async_computation.4 | async-start | bytes 3014656 | tf_op jit(solution)/shard_map/all_to_all | solution.py:43
  288.4 6.3 %fusion.8 = f32[176,1024]{1,0:T(8,128)} fusion(bf16[176,4096]{1,0:T(8,128)(2,1)} %get-tuple-element.72, bf16[4096,2048]{1,0:T(8,128)(2,1)} %all-gather.6.cloned.1.call-done), kind=kOutput, calls=%fused_computation.8 | convolution fusion | flops 1476395008 | bytes 10551296 | tf_op jit(solution)/shard_map/dot_general | solution.py:35
  302.4 3.9 %split_heads.1 = (f32[64,16,64]{2,1,0:T(8,128)}, f32[64,16,64]{2,1,0:T(8,128)}, f32[64,16,64]{2,1,0:T(8,128)}) custom-call(f32[16,96,128]{2,1,0:T(8,128)} %copy-done.3), custom_call_target="tpu_custom_call" | custom-call | tf_op jit(solution)/shard_map/split_heads/pallas_call | solution.py:449
  306.3 7.0 %collective-permute-done.1 = f32[64,1024]{1,0:T(8,128)S(1)} collective-permute-done((f32[64,1024]{1,0:T(8,128)S(1)}, f32[64,1024]{1,0:T(8,128)S(1)}, u32[]{:S(2)}, u32[]{:S(2)}) %collective-permute-start.1) | collective-permute-done | bytes 262176 | tf_op jit(solution)/shard_map/ppermute | solution.py:580
  315.2 3.3 %join_columns.1 = (f32[64,2816]{1,0:T(8,128)}, f32[64,2816]{1,0:T(8,128)}) custom-call(f32[16,184,128]{2,1,0:T(8,128)} %copy-done), custom_call_target="tpu_custom_call" | custom-call | tf_op jit(solution)/shard_map/join_columns/pallas_call | solution.py:434
  (125 shorter events, 56.4 us)
Async XLA Ops:
  7.2 116.2 %all-gather.4.cloned.1.call-start = ((), (), s32[]{:S(2)}) async-start(), calls=%async_computation.5 | async-start | bytes 21168128 | tf_op jit(solution)/shard_map/all_gather | solution.py:39
  91.0 28.1 %copy-start.7 = (bf16[64,4096]{1,0:T(8,128)(2,1)S(1)}, bf16[64,4096]{1,0:T(8,128)(2,1)}, u32[]{:S(2)}) copy-start(bf16[64,4096]{1,0:T(8,128)(2,1)} %slice.201.refs_2_) | copy-start | bytes 1572868
  114.5 15.7 %all-to-all-start = ((bf16[16,64,256]{2,1,0:T(8,128)(2,1)}), bf16[16,64,256]{2,1,0:T(8,128)(2,1)S(1)}, u32[]{:S(2)}, u32[]{:S(2)}) async-start(bf16[16,64,256]{2,1,0:T(8,128)(2,1)} %get-tuple-element.78), calls=%async_computation | async-start | bytes 1048576 | tf_op jit(solution)/shard_map/all_to_all | solution.py:43
  118.7 141.0 %all-gather.6.cloned.1.call-start = ((), (), s32[]{:S(2)}) async-start(), calls=%async_computation.6 | async-start | bytes 17825792 | tf_op jit(solution)/shard_map/all_gather | solution.py:39
  127.0 4.0 %copy-start.5 = (bf16[256,1024]{1,0:T(8,128)(2,1)S(1)}, bf16[256,1024]{1,0:T(8,128)(2,1)}, u32[]{:S(2)}) copy-start(bf16[256,1024]{1,0:T(8,128)(2,1)} %refs_0_.1) | copy-start | bytes 1572868
  130.2 4.4 %copy-start.9 = (bf16[256,1024]{1,0:T(8,128)(2,1)S(1)}, bf16[256,1024]{1,0:T(8,128)(2,1)}, u32[]{:S(2)}) copy-start(bf16[256,1024]{1,0:T(8,128)(2,1)} %param.14) | copy-start | bytes 1572868
  135.7 6.4 %slice-start = ((s8[5767168]{0:T(1024)(128)(4,1)}), s8[1572864]{0:T(1024)(128)(4,1)S(1)}, s32[]{:S(2)}) async-start(s8[5767168]{0:T(1024)(128)(4,1)} %bitcast.59), calls=%async_computation.8 | async-start | bytes 3145728
  135.7 6.3 %slice-start.1 = ((s8[5767168]{0:T(1024)(128)(4,1)}), s8[4194304]{0:T(1024)(128)(4,1)S(1)}, s32[]{:S(2)}) async-start(s8[5767168]{0:T(1024)(128)(4,1)} %bitcast.59), calls=%async_computation.9 | async-start | bytes 8388608
  152.7 7.4 %copy-start.1 = (bf16[256,1024]{1,0:T(8,128)(2,1)}, bf16[256,1024]{1,0:T(8,128)(2,1)S(1)}, u32[]{:S(2)}) copy-start(bf16[256,1024]{1,0:T(8,128)(2,1)S(1)} %fusion.56) | copy-start | bytes 1572868
  156.0 20.0 %all-to-all-start.1 = ((bf16[16,64,256]{2,1,0:T(8,128)(2,1)}), bf16[16,64,256]{2,1,0:T(8,128)(2,1)S(1)}, u32[]{:S(2)}, u32[]{:S(2)}) async-start(bf16[16,64,256]{2,1,0:T(8,128)(2,1)} %bitcast.13), calls=%async_computation.1 | async-start | bytes 1048576 | tf_op jit(solution)/shard_map/all_to_all | solution.py:43
  159.5 135.3 %all-gather.8.cloned.1.call-start = ((), (), s32[]{:S(2)}) async-start(), calls=%async_computation.7 | async-start | bytes 4718592 | tf_op jit(solution)/shard_map/all_gather | solution.py:550
  223.3 3.8 %copy-start.6 = (bf16[16,64,256]{2,1,0:T(8,128)(2,1)S(1)}, bf16[16,64,256]{2,1,0:T(8,128)(2,1)}, u32[]{:S(2)}) copy-start(bf16[16,64,256]{2,1,0:T(8,128)(2,1)} %get-tuple-element.78) | copy-start | bytes 1572868
  223.3 27.3 %all-to-all-start.2 = ((bf16[16,192,256]{2,1,0:T(8,128)(2,1)}), bf16[16,192,256]{2,1,0:T(8,128)(2,1)S(1)}, u32[]{:S(2)}, u32[]{:S(2)}) async-start(bf16[16,192,256]{2,1,0:T(8,128)(2,1)} %get-tuple-element.62), calls=%async_computation.2 | async-start | bytes 3145728 | tf_op jit(solution)/shard_map/all_to_all | solution.py:43
  227.8 66.9 %collective-permute-start = (bf16[8,64,256]{2,1,0:T(8,128)(2,1)}, bf16[8,64,256]{2,1,0:T(8,128)(2,1)}, u32[]{:S(2)}, u32[]{:S(2)}) collective-permute-start(bf16[8,64,256]{2,1,0:T(8,128)(2,1)} %constant_dynamic-slice_fusion.1), channel_id=1, source_target_pairs={{0,8},{1,9},{2,10},{3,11},{4,12},{5,13},{6,14},{7,15},{8,0},{9,1},... | collective-permute-start | bytes 786440 | tf_op jit(solution)/shard_map/ppermute | solution.py:548
  254.6 5.1 %copy-start.16 = (bf16[1024,176]{1,0:T(8,128)(2,1)S(1)}, bf16[1024,176]{1,0:T(8,128)(2,1)}, u32[]{:S(2)}) copy-start(bf16[1024,176]{1,0:T(8,128)(2,1)} %get-tuple-element.95) | copy-start | bytes 1081348
  254.6 5.1 %copy-start.17 = (bf16[1024,176]{1,0:T(8,128)(2,1)S(1)}, bf16[1024,176]{1,0:T(8,128)(2,1)}, u32[]{:S(2)}) copy-start(bf16[1024,176]{1,0:T(8,128)(2,1)} %get-tuple-element.96) | copy-start | bytes 1081348
  256.5 27.9 %all-to-all-start.3 = ((f32[16,96,128]{2,1,0:T(8,128)}), f32[16,96,128]{2,1,0:T(8,128)S(1)}, u32[]{:S(2)}, u32[]{:S(2)}) async-start(f32[16,96,128]{2,1,0:T(8,128)} %pack_pairs.2), calls=%async_computation.3 | async-start | bytes 1572864 | tf_op jit(solution)/shard_map/all_to_all | solution.py:43
  259.7 10.5 %copy-start.18 = (bf16[176,1024]{1,0:T(8,128)(2,1)S(1)}, bf16[176,1024]{1,0:T(8,128)(2,1)}, u32[]{:S(2)}) copy-start(bf16[176,1024]{1,0:T(8,128)(2,1)} %down.1) | copy-start | bytes 1081348
  259.7 10.5 %copy-start.20 = (bf16[4096,2048]{1,0:T(8,128)(2,1)S(1)}, bf16[4096,2048]{1,0:T(8,128)(2,1)}, u32[]{:S(2)}) copy-start(bf16[4096,2048]{1,0:T(8,128)(2,1)} %all-gather.6.cloned.1.call-done) | copy-start | bytes 50331652
  284.3 10.5 %copy-start.3 = (f32[16,96,128]{2,1,0:T(8,128)}, f32[16,96,128]{2,1,0:T(8,128)S(1)}, u32[]{:S(2)}) copy-start(f32[16,96,128]{2,1,0:T(8,128)S(1)} %all-to-all-done.3.refs_0_) | copy-start | bytes 2359300
  284.3 29.7 %all-to-all-start.4 = ((f32[16,184,128]{2,1,0:T(8,128)}), f32[16,184,128]{2,1,0:T(8,128)S(1)}, u32[]{:S(2)}, u32[]{:S(2)}) async-start(f32[16,184,128]{2,1,0:T(8,128)} %pack_pairs.3), calls=%async_computation.4 | async-start | bytes 3014656 | tf_op jit(solution)/shard_map/all_to_all | solution.py:43
  296.1 5.1 %copy-start.2 = (bf16[256,1024]{1,0:T(8,128)(2,1)S(1)}, bf16[256,1024]{1,0:T(8,128)(2,1)}, u32[]{:S(2)}) copy-start(bf16[256,1024]{1,0:T(8,128)(2,1)} %copy-done.1) | copy-start | bytes 1572868
  296.1 5.1 %copy-start.14 = (bf16[256,1024]{1,0:T(8,128)(2,1)S(1)}, bf16[256,1024]{1,0:T(8,128)(2,1)}, u32[]{:S(2)}) copy-start(bf16[256,1024]{1,0:T(8,128)(2,1)} %get-tuple-element.125) | copy-start | bytes 1572868
  299.2 14.1 %collective-permute-start.1 = (f32[64,1024]{1,0:T(8,128)S(1)}, f32[64,1024]{1,0:T(8,128)S(1)}, u32[]{:S(2)}, u32[]{:S(2)}) collective-permute-start(f32[64,1024]{1,0:T(8,128)S(1)} %slice.135), channel_id=1, source_target_pairs={{0,8},{1,9},{2,10},{3,11},{4,12},{5,13},{6,14},{7,15},{8,0},{9,1},... | collective-permute-start | bytes 786440 | tf_op jit(solution)/shard_map/ppermute | solution.py:580
  (13 other events, 23.2 us)
Sparse Core Ops, SparseCore 0:
  10.2 113.1 all-gather.3
  135.8 104.1 all-gather.5
  242.5 40.7 all-gather.7
where the time goes:
time: 332 us; the launch traced here: 327 us
  Pallas kernels  153 us (46%)
  matrix products  70.1 us (21%)
  waiting for transfers between devices  25.5 us (8%)
  starting transfers between devices  22.8 us (7%)
  local copies, waits for them, and re-layouts  22.7 us (7%)
  other arithmetic  18.3 us (6%)
  between operations  14.4 us (4%)
    dot_general x15, matrix products, dot(): lax.dot_general(lhs, rhs, (((l_dim,), (r_dim,)), ((), ())), preferred_ele...  70.1 us
    pallas_call x1, Pallas kernels, gather_proj(): pl.pallas_call(lambda *refs: gather_proj_kernel(n_dev, *refs), in_specs=[...  67.8 us
    pallas_call x1, Pallas kernels, attention_bwd(): pl.pallas_call(lambda *refs: attn_bwd_kernel(n_blocks, TILE, block, *refs...  46.5 us
    pallas_call x1, Pallas kernels, attention_fwd(): pl.pallas_call(lambda *refs: attn_fwd_kernel(TILE, *refs), grid=(seq // T...  23.6 us
    all_to_all x5, starting transfers between devices, exchange(): return lax.all_to_all(blocks, SEQ_AXIS, 0, 0, tiled=True)  17.9 us
    all_to_all x5, waiting for transfers between devices, exchange(): return lax.all_to_all(blocks, SEQ_AXIS, 0, 0, tiled=True)  17.8 us
    ppermute x1, waiting for transfers between devices, device_step(): lax.ppermute(part_w_o[head_dim:], SEQ_AXIS, pairs)  6.97 us
    unnamed x58, local copies, waits for them, and re-layouts  6.67 us
  transfers between devices with their start and end apart: 10, of which 4 were waited for; matrix products, arithmetic and copies ran while one was open for 31% of the time, Pallas kernels for 45%

commit v1 on v0

--- a/solution.py
+++ b/solution.py
@@ -553,7 +553,8 @@
     d_blocks, d_proj_t, *w_qkv_all = attention_bwd(q_t, do_t, of_t, lse, k_in, k_t, v_in, cos_t, sin_t, w_parts, n_dev)
     d_proj = exchange(d_blocks)
 
-    attn_send = pack_pairs(dot(d_proj_t, u_all, 1, 0), n_dev, rows)
+    grad_w_qkv = dot(d_proj_t, u_all, 1, 0)
+    attn_send = pack_pairs(grad_w_qkv, n_dev, rows)
     d_proj, attn_send = lax.optimization_barrier((d_proj, attn_send))
     attn_back = exchange(attn_send)
     d_proj = d_proj.reshape(heads, 3, head_dim, tok)
@@ -569,7 +570,8 @@
     d_mixed_t = dot(w_down, dy_all, 1, 1).astype(BF16).astype(F32)
     mixed_t = (jax.nn.silu(gate_t) * up_t).astype(BF16)
     d_gu_t = jnp.concatenate(gate_backward(d_mixed_t, gate_t, up_t), axis=0)
-    mlp_send = pack_pairs(dot(d_gu_t, a_all, 1, 0), n_dev, rows, jnp.pad(gain_send, ((0, 0), (0, 7), (0, 0))))
+    grad_w_gu = dot(d_gu_t, a_all, 1, 0)
+    mlp_send = pack_pairs(grad_w_gu, n_dev, rows, jnp.pad(gain_send, ((0, 0), (0, 7), (0, 0))))
     attn_back, mlp_send, mixed_t = lax.optimization_barrier((attn_back, mlp_send, mixed_t))
     mlp_back = exchange(mlp_send)
     grad_w_down = dot(mixed_t, dy_all, 1, 0)

time: 332 us -> 332 us (level)
  no operation moved by 1% of the time
where the time goes in v1:
time: 332 us; the launch traced here: 327 us
  Pallas kernels  153 us (46%)
  matrix products  70.1 us (21%)
  waiting for transfers between devices  25.5 us (8%)
  starting transfers between devices  22.8 us (7%)
  local copies, waits for them, and re-layouts  22.7 us (7%)
  other arithmetic  18.3 us (6%)
  between operations  14.4 us (4%)
    dot_general x15, matrix products, dot(): lax.dot_general(lhs, rhs, (((l_dim,), (r_dim,)), ((), ())), preferred_ele...  70.1 us
    pallas_call x1, Pallas kernels, gather_proj(): pl.pallas_call(lambda *refs: gather_proj_kernel(n_dev, *refs), in_specs=[...  67.8 us
    pallas_call x1, Pallas kernels, attention_bwd(): pl.pallas_call(lambda *refs: attn_bwd_kernel(n_blocks, TILE, block, *refs...  46.5 us
    pallas_call x1, Pallas kernels, attention_fwd(): pl.pallas_call(lambda *refs: attn_fwd_kernel(TILE, *refs), grid=(seq // T...  23.6 us
    all_to_all x5, starting transfers between devices, exchange(): return lax.all_to_all(blocks, SEQ_AXIS, 0, 0, tiled=True)  17.9 us
    all_to_all x5, waiting for transfers between devices, exchange(): return lax.all_to_all(blocks, SEQ_AXIS, 0, 0, tiled=True)  17.8 us
    ppermute x1, waiting for transfers between devices, device_step(): lax.ppermute(part_w_o[head_dim:], SEQ_AXIS, pairs)  6.97 us
    unnamed x58, local copies, waits for them, and re-layouts  6.67 us
  transfers between devices with their start and end apart: 10, of which 4 were waited for; matrix products, arithmetic and copies ran while one was open for 31% of the time, Pallas kernels for 45%

profile of v1, /device:TPU:0, one launch (start us, length us, event | category | flops | bytes accessed | tf_op | source)
XLA Modules:
  0.0 326.7 jit_solution(11074867505769132570)
XLA Ops:
  11.8 67.8 %gather_proj.1 = (bf16[16,256,1024]{2,1,0:T(8,128)(2,1)}, f32[192,4096]{1,0:T(8,128)}, f32[16,8,128]{2,1,0:T(8,128)}) custom-call(bf16[256,1024]{1,0:T(8,128)(2,1)} %refs_0_.1, f32[8,128]{1,0:T(8,128)} %select_maximum_fusion.1.refs_1_, bf16[16,64,256]{2,1,0:T(8,128)(2,1)} %pad.13.refs_2_), custom_call_target="tpu_custom_call" | custom-call | flops 128849018880 | bytes 16777216 | tf_op jit(solution)/shard_map/gather_proj/pallas_call | solution.py:395
  82.6 5.3 %fusion.85 = (bf16[32,4096]{1,0:T(8,128)(2,1)S(1)}, bf16[32,4096]{1,0:T(8,128)(2,1)S(1)}, bf16[32,4096]{1,0:T(8,128)(2,1)S(1)}, bf16[32,4096]{1,0:T(8,128)(2,1)S(1)}, f32[32,4096]{1,0:T(8,128)}, /*index=5*/f32[32,4096]{1,0:T(8,128)}) fusion(f32[192,4096]{1,0:T(8,128)} %get-tuple-element.50, f32[4096]{0:T(1024)S(1)} %bitcast.72, f32[32]{0:T(128)S(1)} %negate_power_fusion), kind=kLoop, calls=%fused_computation.100 | loop fusion | flops 2228224 | bytes 4210816 | tf_op jit(solution)/shard_map/convert.3
  91.0 23.6 %attn_fwd.1 = (bf16[16,64,256]{2,1,0:T(8,128)(2,1)}, f32[64,4096]{1,0:T(8,128)}, f32[1,4096]{1,0:T(1,128)}) custom-call(bf16[64,4096]{1,0:T(8,128)(2,1)} %multiply_convert_fusion.11.refs_0_, bf16[4096,64]{1,0:T(8,128)(2,1)} %copy.56.refs_1_.refs_6_, bf16[64,4096]{1,0:T(8,128)(2,1)} %slice.201.refs_2_), custom_call_target="tpu_custom_call" | custom-call | flops 8589934592 | bytes 2097152 | tf_op jit(solution)/shard_map/attn_fwd/pallas_call | solution.py:96
  114.5 4.1 %all-to-all-start = ((bf16[16,64,256]{2,1,0:T(8,128)(2,1)}), bf16[16,64,256]{2,1,0:T(8,128)(2,1)S(1)}, u32[]{:S(2)}, u32[]{:S(2)}) async-start(bf16[16,64,256]{2,1,0:T(8,128)(2,1)} %get-tuple-element.78), calls=%async_computation | async-start | bytes 1048576 | tf_op jit(solution)/shard_map/all_to_all | solution.py:43
  123.4 3.6 %fusion.94 = (bf16[1024,1024]{1,0:T(8,128)(2,1)S(1)}, bf16[1024,1024]{1,0:T(8,128)(2,1)S(1)}, bf16[1024,1024]{1,0:T(8,128)(2,1)S(1)}) fusion(bf16[1024,9728]{1,0:T(8,128)(2,1)} %all-gather.4.cloned.1.call-done), kind=kLoop, calls=%fused_computation.134 | loop fusion | bytes 12582912 | tf_op jit(solution)/shard_map/slice | solution.py:510
  127.0 3.2 pad_maximum_fusion
  135.7 6.3 %fusion.2 = f32[256,5632]{1,0:T(8,128)S(1)} fusion(bf16[256,1024]{1,0:T(8,128)(2,1)} %copy-done.10, bf16[1024,9728]{1,0:T(8,128)(2,1)} %all-gather.4.cloned.1.call-done), kind=kOutput, calls=%fused_computation.2 | convolution fusion | flops 2952790016 | bytes 17825792 | tf_op jit(solution)/shard_map/dot_general | solution.py:35
  144.7 7.6 %fusion.68 = (f32[1024]{0:T(1024)S(1)}, f32[256]{0:T(256)S(1)}, bf16[256,1024]{1,0:T(8,128)(2,1)S(1)}) fusion(bf16[256,1024]{1,0:T(8,128)(2,1)S(1)} %get-tuple-element.123, f32[256]{0:T(256)S(1)} %get-tuple-element.119, f32[1024]{0:T(1024)S(1)} %mul.270, bf16[1024,9728]{1,0:T(8,128)(2,1)} %all-gather.4.cloned.1.call-done, ...), kind=kOutput, calls=%fused_computation.78 | convolution fusion | flops 2960915200 | bytes 15476736 | tf_op jit(solution)/shard_map/dot_general | solution.py:35
  152.7 3.3 %fusion.45 = bf16[1024,256]{1,0:T(8,128)(2,1)} fusion(bf16[256,1024]{1,0:T(8,128)(2,1)S(1)} %fusion.56, bf16[1024,9728]{1,0:T(8,128)(2,1)} %all-gather.4.cloned.1.call-done), kind=kOutput, calls=%fused_computation.57 | convolution fusion | flops 537133056 | bytes 3145728 | tf_op jit(solution)/shard_map/dot_general | solution.py:35
  156.0 3.4 %all-to-all-start.1 = ((bf16[16,64,256]{2,1,0:T(8,128)(2,1)}), bf16[16,64,256]{2,1,0:T(8,128)(2,1)S(1)}, u32[]{:S(2)}, u32[]{:S(2)}) async-start(bf16[16,64,256]{2,1,0:T(8,128)(2,1)} %bitcast.13), calls=%async_computation.1 | async-start | bytes 1048576 | tf_op jit(solution)/shard_map/all_to_all | solution.py:43
  160.2 6.9 %fusion.39 = bf16[256,1024]{1,0:T(8,128)(2,1)} fusion(bf16[2816,1024]{1,0:T(8,128)(2,1)} %bitcast.58, f32[256,5632]{1,0:T(8,128)} %copy-done.24, bf16[256,1024]{1,0:T(8,128)(2,1)S(1)} %get-tuple-element.123), kind=kOutput, calls=%fused_computation.55 | convolution fusion | flops 1481506816 | bytes 12582912 | tf_op jit(solution)/shard_map/dot_general | solution.py:35
  167.1 8.9 %all-to-all-done.1 = bf16[16,64,256]{2,1,0:T(8,128)(2,1)S(1)} async-done(((bf16[16,64,256]{2,1,0:T(8,128)(2,1)}), bf16[16,64,256]{2,1,0:T(8,128)(2,1)S(1)}, u32[]{:S(2)}, u32[]{:S(2)}) %all-to-all-start.1) | async-done | bytes 524320 | tf_op jit(solution)/shard_map/all_to_all | solution.py:43
  176.9 46.5 %attn_bwd.1 = (bf16[16,192,256]{2,1,0:T(8,128)(2,1)}, bf16[192,4096]{1,0:T(8,128)(2,1)}, bf16[16,64,1024]{2,1,0:T(8,128)(2,1)}, bf16[16,64,1024]{2,1,0:T(8,128)(2,1)}, bf16[16,64,1024]{2,1,0:T(8,128)(2,1)}) custom-call(bf16[64,4096]{1,0:T(8,128)(2,1)} %multiply_convert_fusion.11.refs_0_, bf16[64,4096]{1,0:T(8,128)(2,1)} %bitcast.70, ...), custom_call_target="tpu_custom_call" | custom-call | flops 21474836480 | bytes 5242880 | tf_op jit(solution)/shard_map/attn_bwd/pallas_call | solution.py:278
  223.3 3.7 %all-to-all-start.2 = ((bf16[16,192,256]{2,1,0:T(8,128)(2,1)}), bf16[16,192,256]{2,1,0:T(8,128)(2,1)S(1)}, u32[]{:S(2)}, u32[]{:S(2)}) async-start(bf16[16,192,256]{2,1,0:T(8,128)(2,1)} %get-tuple-element.62), calls=%async_computation.2 | async-start | bytes 3145728 | tf_op jit(solution)/shard_map/all_to_all | solution.py:43
  232.9 6.6 %fusion.97.refs_0_ = f32[192,1024]{1,0:T(8,128)} fusion(bf16[192,4096]{1,0:T(8,128)(2,1)} %get-tuple-element.63, bf16[4096,1024]{1,0:T(8,128)(2,1)} %bitcast.75), kind=kOutput, calls=%fused_computation.137 | convolution fusion | flops 1610612736 | bytes 10747904 | tf_op jit(solution)/shard_map/dot_general | solution.py:35
  241.8 8.9 %all-to-all-done.2 = bf16[16,192,256]{2,1,0:T(8,128)(2,1)S(1)} async-done(((bf16[16,192,256]{2,1,0:T(8,128)(2,1)}), bf16[16,192,256]{2,1,0:T(8,128)(2,1)S(1)}, u32[]{:S(2)}, u32[]{:S(2)}) %all-to-all-start.2) | async-done | bytes 1572896 | tf_op jit(solution)/shard_map/all_to_all | solution.py:43
  259.7 10.5 %fusion.6 = f32[352,4096]{1,0:T(8,128)} fusion(bf16[4096,2048]{1,0:T(8,128)(2,1)} %all-gather.6.cloned.1.call-done, bf16[1024,176]{1,0:T(8,128)(2,1)S(1)} %copy-done.17, bf16[1024,176]{1,0:T(8,128)(2,1)S(1)} %copy-done.16), kind=kOutput, calls=%fused_computation.6 | convolution fusion | flops 2954231808 | bytes 14876672 | tf_op jit(solution)/shard_map/dot_general | solution.py:35
  270.2 6.8 %multiply_convert_fusion.2 = (bf16[176,4096]{1,0:T(8,128)(2,1)S(1)}, bf16[176,4096]{1,0:T(8,128)(2,1)S(1)}, bf16[176,4096]{1,0:T(8,128)(2,1)}) fusion(f32[352,4096]{1,0:T(8,128)} %fusion.6, bf16[176,1024]{1,0:T(8,128)(2,1)S(1)} %copy-done.18, bf16[4096,2048]{1,0:T(8,128)(2,1)S(1)} %copy-done.20), kind=kOutput, calls=%fused_computation.28 | convolution fusion | flops 1489371136 | bytes 18841600 | tf_op jit(solution)/shard_map/dot_general | solution.py:35
  277.0 4.3 %fusion.4.refs_0_ = f32[352,1024]{1,0:T(8,128)} fusion(bf16[4096,2048]{1,0:T(8,128)(2,1)S(1)} %copy-done.20, bf16[176,4096]{1,0:T(8,128)(2,1)S(1)} %get-tuple-element.101, bf16[176,4096]{1,0:T(8,128)(2,1)S(1)} %get-tuple-element.100), kind=kOutput, calls=%fused_computation.4 | convolution fusion | flops 2958557184 | bytes 12713984 | tf_op jit(solution)/shard_map/dot_general | solution.py:35
  284.3 4.1 %all-to-all-start.4 = ((f32[16,184,128]{2,1,0:T(8,128)}), f32[16,184,128]{2,1,0:T(8,128)S(1)}, u32[]{:S(2)}, u32[]{:S(2)}) async-start(f32[16,184,128]{2,1,0:T(8,128)} %pack_pairs.3), calls=%async_computation.4 | async-start | bytes 3014656 | tf_op jit(solution)/shard_map/all_to_all | solution.py:43
  288.4 6.3 %fusion.8 = f32[176,1024]{1,0:T(8,128)} fusion(bf16[176,4096]{1,0:T(8,128)(2,1)} %get-tuple-element.72, bf16[4096,2048]{1,0:T(8,128)(2,1)} %all-gather.6.cloned.1.call-done), kind=kOutput, calls=%fused_computation.8 | convolution fusion | flops 1476395008 | bytes 10551296 | tf_op jit(solution)/shard_map/dot_general | solution.py:35
  302.4 3.9 %split_heads.1 = (f32[64,16,64]{2,1,0:T(8,128)}, f32[64,16,64]{2,1,0:T(8,128)}, f32[64,16,64]{2,1,0:T(8,128)}) custom-call(f32[16,96,128]{2,1,0:T(8,128)} %copy-done.3), custom_call_target="tpu_custom_call" | custom-call | tf_op jit(solution)/shard_map/split_heads/pallas_call | solution.py:449
  306.3 7.0 %collective-permute-done.1 = f32[64,1024]{1,0:T(8,128)S(1)} collective-permute-done((f32[64,1024]{1,0:T(8,128)S(1)}, f32[64,1024]{1,0:T(8,128)S(1)}, u32[]{:S(2)}, u32[]{:S(2)}) %collective-permute-start.1) | collective-permute-done | bytes 262176 | tf_op jit(solution)/shard_map/ppermute | solution.py:582
  315.2 3.3 %join_columns.1 = (f32[64,2816]{1,0:T(8,128)}, f32[64,2816]{1,0:T(8,128)}) custom-call(f32[16,184,128]{2,1,0:T(8,128)} %copy-done), custom_call_target="tpu_custom_call" | custom-call | tf_op jit(solution)/shard_map/join_columns/pallas_call | solution.py:434
  (125 shorter events, 56.4 us)
Async XLA Ops:
  7.2 116.2 %all-gather.4.cloned.1.call-start = ((), (), s32[]{:S(2)}) async-start(), calls=%async_computation.5 | async-start | bytes 21168128 | tf_op jit(solution)/shard_map/all_gather | solution.py:39
  91.0 28.1 %copy-start.7 = (bf16[64,4096]{1,0:T(8,128)(2,1)S(1)}, bf16[64,4096]{1,0:T(8,128)(2,1)}, u32[]{:S(2)}) copy-start(bf16[64,4096]{1,0:T(8,128)(2,1)} %slice.201.refs_2_) | copy-start | bytes 1572868
  114.5 15.7 %all-to-all-start = ((bf16[16,64,256]{2,1,0:T(8,128)(2,1)}), bf16[16,64,256]{2,1,0:T(8,128)(2,1)S(1)}, u32[]{:S(2)}, u32[]{:S(2)}) async-start(bf16[16,64,256]{2,1,0:T(8,128)(2,1)} %get-tuple-element.78), calls=%async_computation | async-start | bytes 1048576 | tf_op jit(solution)/shard_map/all_to_all | solution.py:43
  118.7 141.0 %all-gather.6.cloned.1.call-start = ((), (), s32[]{:S(2)}) async-start(), calls=%async_computation.6 | async-start | bytes 17825792 | tf_op jit(solution)/shard_map/all_gather | solution.py:39
  127.0 4.0 %copy-start.5 = (bf16[256,1024]{1,0:T(8,128)(2,1)S(1)}, bf16[256,1024]{1,0:T(8,128)(2,1)}, u32[]{:S(2)}) copy-start(bf16[256,1024]{1,0:T(8,128)(2,1)} %refs_0_.1) | copy-start | bytes 1572868
  130.2 4.4 %copy-start.9 = (bf16[256,1024]{1,0:T(8,128)(2,1)S(1)}, bf16[256,1024]{1,0:T(8,128)(2,1)}, u32[]{:S(2)}) copy-start(bf16[256,1024]{1,0:T(8,128)(2,1)} %param.14) | copy-start | bytes 1572868
  135.7 6.4 %slice-start = ((s8[5767168]{0:T(1024)(128)(4,1)}), s8[1572864]{0:T(1024)(128)(4,1)S(1)}, s32[]{:S(2)}) async-start(s8[5767168]{0:T(1024)(128)(4,1)} %bitcast.59), calls=%async_computation.8 | async-start | bytes 3145728
  135.7 6.3 %slice-start.1 = ((s8[5767168]{0:T(1024)(128)(4,1)}), s8[4194304]{0:T(1024)(128)(4,1)S(1)}, s32[]{:S(2)}) async-start(s8[5767168]{0:T(1024)(128)(4,1)} %bitcast.59), calls=%async_computation.9 | async-start | bytes 8388608
  152.7 7.4 %copy-start.1 = (bf16[256,1024]{1,0:T(8,128)(2,1)}, bf16[256,1024]{1,0:T(8,128)(2,1)S(1)}, u32[]{:S(2)}) copy-start(bf16[256,1024]{1,0:T(8,128)(2,1)S(1)} %fusion.56) | copy-start | bytes 1572868
  156.0 20.0 %all-to-all-start.1 = ((bf16[16,64,256]{2,1,0:T(8,128)(2,1)}), bf16[16,64,256]{2,1,0:T(8,128)(2,1)S(1)}, u32[]{:S(2)}, u32[]{:S(2)}) async-start(bf16[16,64,256]{2,1,0:T(8,128)(2,1)} %bitcast.13), calls=%async_computation.1 | async-start | bytes 1048576 | tf_op jit(solution)/shard_map/all_to_all | solution.py:43
  159.5 135.3 %all-gather.8.cloned.1.call-start = ((), (), s32[]{:S(2)}) async-start(), calls=%async_computation.7 | async-start | bytes 4718592 | tf_op jit(solution)/shard_map/all_gather | solution.py:550
  223.3 3.8 %copy-start.6 = (bf16[16,64,256]{2,1,0:T(8,128)(2,1)S(1)}, bf16[16,64,256]{2,1,0:T(8,128)(2,1)}, u32[]{:S(2)}) copy-start(bf16[16,64,256]{2,1,0:T(8,128)(2,1)} %get-tuple-element.78) | copy-start | bytes 1572868
  223.3 27.3 %all-to-all-start.2 = ((bf16[16,192,256]{2,1,0:T(8,128)(2,1)}), bf16[16,192,256]{2,1,0:T(8,128)(2,1)S(1)}, u32[]{:S(2)}, u32[]{:S(2)}) async-start(bf16[16,192,256]{2,1,0:T(8,128)(2,1)} %get-tuple-element.62), calls=%async_computation.2 | async-start | bytes 3145728 | tf_op jit(solution)/shard_map/all_to_all | solution.py:43
  227.8 66.9 %collective-permute-start = (bf16[8,64,256]{2,1,0:T(8,128)(2,1)}, bf16[8,64,256]{2,1,0:T(8,128)(2,1)}, u32[]{:S(2)}, u32[]{:S(2)}) collective-permute-start(bf16[8,64,256]{2,1,0:T(8,128)(2,1)} %constant_dynamic-slice_fusion.1), channel_id=1, source_target_pairs={{0,8},{1,9},{2,10},{3,11},{4,12},{5,13},{6,14},{7,15},{8,0},{9,1},... | collective-permute-start | bytes 786440 | tf_op jit(solution)/shard_map/ppermute | solution.py:548
  254.6 5.1 %copy-start.16 = (bf16[1024,176]{1,0:T(8,128)(2,1)S(1)}, bf16[1024,176]{1,0:T(8,128)(2,1)}, u32[]{:S(2)}) copy-start(bf16[1024,176]{1,0:T(8,128)(2,1)} %get-tuple-element.95) | copy-start | bytes 1081348
  254.6 5.1 %copy-start.17 = (bf16[1024,176]{1,0:T(8,128)(2,1)S(1)}, bf16[1024,176]{1,0:T(8,128)(2,1)}, u32[]{:S(2)}) copy-start(bf16[1024,176]{1,0:T(8,128)(2,1)} %get-tuple-element.96) | copy-start | bytes 1081348
  256.5 27.9 %all-to-all-start.3 = ((f32[16,96,128]{2,1,0:T(8,128)}), f32[16,96,128]{2,1,0:T(8,128)S(1)}, u32[]{:S(2)}, u32[]{:S(2)}) async-start(f32[16,96,128]{2,1,0:T(8,128)} %pack_pairs.2), calls=%async_computation.3 | async-start | bytes 1572864 | tf_op jit(solution)/shard_map/all_to_all | solution.py:43
  259.7 10.5 %copy-start.18 = (bf16[176,1024]{1,0:T(8,128)(2,1)S(1)}, bf16[176,1024]{1,0:T(8,128)(2,1)}, u32[]{:S(2)}) copy-start(bf16[176,1024]{1,0:T(8,128)(2,1)} %down.1) | copy-start | bytes 1081348
  259.7 10.5 %copy-start.20 = (bf16[4096,2048]{1,0:T(8,128)(2,1)S(1)}, bf16[4096,2048]{1,0:T(8,128)(2,1)}, u32[]{:S(2)}) copy-start(bf16[4096,2048]{1,0:T(8,128)(2,1)} %all-gather.6.cloned.1.call-done) | copy-start | bytes 50331652
  284.3 10.5 %copy-start.3 = (f32[16,96,128]{2,1,0:T(8,128)}, f32[16,96,128]{2,1,0:T(8,128)S(1)}, u32[]{:S(2)}) copy-start(f32[16,96,128]{2,1,0:T(8,128)S(1)} %all-to-all-done.3.refs_0_) | copy-start | bytes 2359300
  284.3 29.7 %all-to-all-start.4 = ((f32[16,184,128]{2,1,0:T(8,128)}), f32[16,184,128]{2,1,0:T(8,128)S(1)}, u32[]{:S(2)}, u32[]{:S(2)}) async-start(f32[16,184,128]{2,1,0:T(8,128)} %pack_pairs.3), calls=%async_computation.4 | async-start | bytes 3014656 | tf_op jit(solution)/shard_map/all_to_all | solution.py:43
  296.1 5.1 %copy-start.2 = (bf16[256,1024]{1,0:T(8,128)(2,1)S(1)}, bf16[256,1024]{1,0:T(8,128)(2,1)}, u32[]{:S(2)}) copy-start(bf16[256,1024]{1,0:T(8,128)(2,1)} %copy-done.1) | copy-start | bytes 1572868
  296.1 5.1 %copy-start.14 = (bf16[256,1024]{1,0:T(8,128)(2,1)S(1)}, bf16[256,1024]{1,0:T(8,128)(2,1)}, u32[]{:S(2)}) copy-start(bf16[256,1024]{1,0:T(8,128)(2,1)} %get-tuple-element.125) | copy-start | bytes 1572868
  299.2 14.1 %collective-permute-start.1 = (f32[64,1024]{1,0:T(8,128)S(1)}, f32[64,1024]{1,0:T(8,128)S(1)}, u32[]{:S(2)}, u32[]{:S(2)}) collective-permute-start(f32[64,1024]{1,0:T(8,128)S(1)} %slice.135), channel_id=1, source_target_pairs={{0,8},{1,9},{2,10},{3,11},{4,12},{5,13},{6,14},{7,15},{8,0},{9,1},... | collective-permute-start | bytes 786440 | tf_op jit(solution)/shard_map/ppermute | solution.py:582
  (13 other events, 23.2 us)
Sparse Core Ops, SparseCore 0:
  10.2 113.1 all-gather.3
  135.8 104.1 all-gather.5
  242.5 40.7 all-gather.7

commit v2 on v1

--- a/solution.py
+++ b/solution.py
@@ -485,6 +485,29 @@
     return pl.pallas_call(weight_block_kernel, out_shape=jax.ShapeDtypeStruct((rows, width), BF16), name='weight_block')(gate, up, w_o, down)
 
 
+def join_down_kernel(start, src, out, sem):
+    rows, width = src.shape[1], out.shape[2]
+    copies = []
+    for i, top in enumerate(range(0, out.shape[1], rows)):
+        height = min(rows, out.shape[1] - top)
+        copies.append(pltpu.make_async_copy(src.at[:, pl.ds(0, height), pl.ds(start + i * width, width)], out.at[:, pl.ds(top, height), :], sem.at[i]))
+    for copy in copies:
+        copy.start()
+    for copy in copies:
+        copy.wait()
+
+
+def join_down(w_all, start, shape):
+    return pl.pallas_call(
+        lambda *refs: join_down_kernel(start, *refs),
+        in_specs=[pl.BlockSpec(memory_space=pl.ANY)],
+        out_specs=pl.BlockSpec(memory_space=pltpu.VMEM),
+        out_shape=jax.ShapeDtypeStruct(shape, BF16),
+        scratch_shapes=[pltpu.SemaphoreType.DMA((pl.cdiv(shape[1], w_all.shape[1]),))],
+        name='join_down',
+    )(w_all)
+
+
 def device_step(n_dev, x_act, positions, grad_out, g_attn_s, w_q, w_k, w_v, w_o, g_mlp_s, w_gate, w_up, w_down):
     tok, width = x_act.shape
     seq = tok * n_dev
@@ -507,8 +530,7 @@
     w_gu = w_all[:, :2 * ff]
     w_o_all = w_all[:, 2 * ff:2 * ff + width]
     w_down_at = 2 * ff + width
-    down_all = [w_all[:, w_down_at + i * width:w_down_at + (i + 1) * width].reshape(n_dev, rows, width) for i in range(pl.cdiv(ff_s, rows))]
-    w_down_all = jnp.concatenate(down_all, axis=1)[:, :ff_s].reshape(ff, width)
+    w_down_all = join_down(w_all.reshape(n_dev, rows, w_all.shape[1]), w_down_at, (n_dev, ff_s, width)).reshape(ff, width)
     me = lax.axis_index(SEQ_AXIS)
     w_cols = jnp.concatenate([lax.dynamic_slice(w_all, (0, at + me * ff_s), (width, ff_s)) for at in (0, ff)], axis=1)
 

time: 332 us -> 331 us (level)
  Pallas kernels: 153 us -> 158 us
  local copies, waits for them, and re-layouts: 22.7 us -> 19.3 us
    pallas_call x0 -> x1, Pallas kernels: none -> 5.26 us  [join_down(): pl.pallas_call(lambda *refs: join_down_kernel(start, *refs), in_specs=[pl...]
    slice x1 -> x0, local copies, waits for them, and re-layouts: 3.58 us -> none  [device_step(): w_all[:, w_down_at + i * width:w_down_at + (i + 1) * width]]
    unnamed x58 -> x60, local copies, waits for them, and re-layouts: 6.67 us -> 6.6 us
  transfers between devices with their start and end apart: 10 -> 10, of which waited for: 4 -> 5; matrix products, arithmetic and copies ran while one was open for 31% -> 29% of each run, Pallas kernels for 45% -> 47%
where the time goes in v2:
time: 331 us; the launch traced here: 325 us
  Pallas kernels  158 us (48%)
  matrix products  70.2 us (21%)
  waiting for transfers between devices  25.7 us (8%)
  starting transfers between devices  22.3 us (7%)
  local copies, waits for them, and re-layouts  19.3 us (6%)
  other arithmetic  15.2 us (5%)
  between operations  14.5 us (4%)
    dot_general x15, matrix products, dot(): lax.dot_general(lhs, rhs, (((l_dim,), (r_dim,)), ((), ())), preferred_ele...  70.2 us
    pallas_call x1, Pallas kernels, gather_proj(): pl.pallas_call(lambda *refs: gather_proj_kernel(n_dev, *refs), in_specs=[...  67.8 us
    pallas_call x1, Pallas kernels, attention_bwd(): pl.pallas_call(lambda *refs: attn_bwd_kernel(n_blocks, TILE, block, *refs...  46.6 us
    pallas_call x1, Pallas kernels, attention_fwd(): pl.pallas_call(lambda *refs: attn_fwd_kernel(TILE, *refs), grid=(seq // T...  23.6 us
    all_to_all x5, waiting for transfers between devices, exchange(): return lax.all_to_all(blocks, SEQ_AXIS, 0, 0, tiled=True)  18.9 us
    all_to_all x5, starting transfers between devices, exchange(): return lax.all_to_all(blocks, SEQ_AXIS, 0, 0, tiled=True)  17.3 us
  transfers between devices with their start and end apart: 10, of which 5 were waited for; matrix products, arithmetic and copies ran while one was open for 29% of the time, Pallas kernels for 47%

profile of v2, /device:TPU:0, one launch (start us, length us, event | category | flops | bytes accessed | tf_op | source)
XLA Modules:
  0.0 325.3 jit_solution(16961089283689921012)
XLA Ops:
  11.8 67.8 %gather_proj.1 = (bf16[16,256,1024]{2,1,0:T(8,128)(2,1)}, f32[192,4096]{1,0:T(8,128)}, f32[16,8,128]{2,1,0:T(8,128)}) custom-call(bf16[256,1024]{1,0:T(8,128)(2,1)} %refs_0_.1, f32[8,128]{1,0:T(8,128)} %select_maximum_fusion.1.refs_1_, bf16[16,64,256]{2,1,0:T(8,128)(2,1)} %pad.13.refs_2_), custom_call_target="tpu_custom_call" | custom-call | flops 128849018880 | bytes 16777216 | tf_op jit(solution)/shard_map/gather_proj/pallas_call | solution.py:395
  82.6 5.3 %fusion.85 = (bf16[32,4096]{1,0:T(8,128)(2,1)S(1)}, bf16[32,4096]{1,0:T(8,128)(2,1)S(1)}, bf16[32,4096]{1,0:T(8,128)(2,1)S(1)}, bf16[32,4096]{1,0:T(8,128)(2,1)S(1)}, f32[32,4096]{1,0:T(8,128)}, /*index=5*/f32[32,4096]{1,0:T(8,128)}) fusion(f32[192,4096]{1,0:T(8,128)} %get-tuple-element.50, f32[4096]{0:T(1024)S(1)} %bitcast.68, f32[32]{0:T(128)S(1)} %negate_power_fusion), kind=kLoop, calls=%fused_computation.98 | loop fusion | flops 2228224 | bytes 4210816 | tf_op jit(solution)/shard_map/convert.3
  91.0 23.6 %attn_fwd.1 = (bf16[16,64,256]{2,1,0:T(8,128)(2,1)}, f32[64,4096]{1,0:T(8,128)}, f32[1,4096]{1,0:T(1,128)}) custom-call(bf16[64,4096]{1,0:T(8,128)(2,1)} %multiply_convert_fusion.11.refs_0_, bf16[4096,64]{1,0:T(8,128)(2,1)} %copy.56.refs_1_.refs_6_, bf16[64,4096]{1,0:T(8,128)(2,1)} %slice.182.refs_2_), custom_call_target="tpu_custom_call" | custom-call | flops 8589934592 | bytes 2097152 | tf_op jit(solution)/shard_map/attn_fwd/pallas_call | solution.py:96
  114.5 4.1 %all-to-all-start = ((bf16[16,64,256]{2,1,0:T(8,128)(2,1)}), bf16[16,64,256]{2,1,0:T(8,128)(2,1)S(1)}, u32[]{:S(2)}, u32[]{:S(2)}) async-start(bf16[16,64,256]{2,1,0:T(8,128)(2,1)} %get-tuple-element.78), calls=%async_computation | async-start | bytes 1048576 | tf_op jit(solution)/shard_map/all_to_all | solution.py:43
  123.4 5.3 %join_down.1 = bf16[16,176,1024]{2,1,0:T(8,128)(2,1)} custom-call(bf16[16,64,9728]{2,1,0:T(8,128)(2,1)} %bitcast.52), custom_call_target="tpu_custom_call" | custom-call | tf_op jit(solution)/shard_map/join_down/pallas_call | solution.py:501
  134.7 6.3 %fusion.2 = f32[256,5632]{1,0:T(8,128)S(1)} fusion(bf16[256,1024]{1,0:T(8,128)(2,1)} %copy-done.11, bf16[1024,9728]{1,0:T(8,128)(2,1)} %all-gather.4.cloned.1.call-done), kind=kOutput, calls=%fused_computation.2 | convolution fusion | flops 2952790016 | bytes 17825792 | tf_op jit(solution)/shard_map/dot_general | solution.py:35
  143.6 7.7 %fusion.68 = (f32[1024]{0:T(1024)S(1)}, f32[256]{0:T(256)S(1)}, bf16[256,1024]{1,0:T(8,128)(2,1)S(1)}) fusion(bf16[256,1024]{1,0:T(8,128)(2,1)S(1)} %get-tuple-element.120, f32[256]{0:T(256)S(1)} %get-tuple-element.116, f32[1024]{0:T(1024)S(1)} %mul.270, bf16[1024,9728]{1,0:T(8,128)(2,1)} %all-gather.4.cloned.1.call-done, ...), kind=kOutput, calls=%fused_computation.76 | convolution fusion | flops 2960915200 | bytes 15476736 | tf_op jit(solution)/shard_map/dot_general | solution.py:35
  151.7 3.3 %fusion.45 = bf16[1024,256]{1,0:T(8,128)(2,1)} fusion(bf16[256,1024]{1,0:T(8,128)(2,1)S(1)} %fusion.56, bf16[1024,9728]{1,0:T(8,128)(2,1)} %all-gather.4.cloned.1.call-done), kind=kOutput, calls=%fused_computation.55 | convolution fusion | flops 537133056 | bytes 3145728 | tf_op jit(solution)/shard_map/dot_general | solution.py:35
  155.0 3.0 all-to-all-start.1
  158.8 6.9 %fusion.39 = bf16[256,1024]{1,0:T(8,128)(2,1)} fusion(bf16[2816,1024]{1,0:T(8,128)(2,1)} %bitcast.54, f32[256,5632]{1,0:T(8,128)} %copy-done.25, bf16[256,1024]{1,0:T(8,128)(2,1)S(1)} %get-tuple-element.120), kind=kOutput, calls=%fused_computation.53 | convolution fusion | flops 1481506816 | bytes 12582912 | tf_op jit(solution)/shard_map/dot_general | solution.py:35
  165.7 8.9 %all-to-all-done.1 = bf16[16,64,256]{2,1,0:T(8,128)(2,1)S(1)} async-done(((bf16[16,64,256]{2,1,0:T(8,128)(2,1)}), bf16[16,64,256]{2,1,0:T(8,128)(2,1)S(1)}, u32[]{:S(2)}, u32[]{:S(2)}) %all-to-all-start.1) | async-done | bytes 524320 | tf_op jit(solution)/shard_map/all_to_all | solution.py:43
  175.4 46.6 %attn_bwd.1 = (bf16[16,192,256]{2,1,0:T(8,128)(2,1)}, bf16[192,4096]{1,0:T(8,128)(2,1)}, bf16[16,64,1024]{2,1,0:T(8,128)(2,1)}, bf16[16,64,1024]{2,1,0:T(8,128)(2,1)}, bf16[16,64,1024]{2,1,0:T(8,128)(2,1)}) custom-call(bf16[64,4096]{1,0:T(8,128)(2,1)} %multiply_convert_fusion.11.refs_0_, bf16[64,4096]{1,0:T(8,128)(2,1)} %bitcast.66, ...), custom_call_target="tpu_custom_call" | custom-call | flops 21474836480 | bytes 5242880 | tf_op jit(solution)/shard_map/attn_bwd/pallas_call | solution.py:278
  222.0 3.6 %all-to-all-start.2 = ((bf16[16,192,256]{2,1,0:T(8,128)(2,1)}), bf16[16,192,256]{2,1,0:T(8,128)(2,1)S(1)}, u32[]{:S(2)}, u32[]{:S(2)}) async-start(bf16[16,192,256]{2,1,0:T(8,128)(2,1)} %get-tuple-element.62), calls=%async_computation.2 | async-start | bytes 3145728 | tf_op jit(solution)/shard_map/all_to_all | solution.py:43
  230.8 6.6 %fusion.96.refs_0_ = f32[192,1024]{1,0:T(8,128)} fusion(bf16[192,4096]{1,0:T(8,128)(2,1)} %get-tuple-element.63, bf16[4096,1024]{1,0:T(8,128)(2,1)} %bitcast.71), kind=kOutput, calls=%fused_computation.134 | convolution fusion | flops 1610612736 | bytes 10747904 | tf_op jit(solution)/shard_map/dot_general | solution.py:35
  239.7 9.5 %all-to-all-done.2 = bf16[16,192,256]{2,1,0:T(8,128)(2,1)S(1)} async-done(((bf16[16,192,256]{2,1,0:T(8,128)(2,1)}), bf16[16,192,256]{2,1,0:T(8,128)(2,1)S(1)}, u32[]{:S(2)}, u32[]{:S(2)}) %all-to-all-start.2) | async-done | bytes 1572896 | tf_op jit(solution)/shard_map/all_to_all | solution.py:43
  258.3 10.5 %fusion.6 = f32[352,4096]{1,0:T(8,128)} fusion(bf16[4096,2048]{1,0:T(8,128)(2,1)} %all-gather.6.cloned.1.call-done, bf16[1024,176]{1,0:T(8,128)(2,1)S(1)} %copy-done.18, bf16[1024,176]{1,0:T(8,128)(2,1)S(1)} %copy-done.17), kind=kOutput, calls=%fused_computation.6 | convolution fusion | flops 2954231808 | bytes 14876672 | tf_op jit(solution)/shard_map/dot_general | solution.py:35
  268.8 6.8 %multiply_convert_fusion.2 = (bf16[176,4096]{1,0:T(8,128)(2,1)S(1)}, bf16[176,4096]{1,0:T(8,128)(2,1)S(1)}, bf16[176,4096]{1,0:T(8,128)(2,1)}) fusion(f32[352,4096]{1,0:T(8,128)} %fusion.6, bf16[176,1024]{1,0:T(8,128)(2,1)S(1)} %copy-done.19, bf16[4096,2048]{1,0:T(8,128)(2,1)S(1)} %copy-done.21), kind=kOutput, calls=%fused_computation.26 | convolution fusion | flops 1489371136 | bytes 18841600 | tf_op jit(solution)/shard_map/dot_general | solution.py:35
  275.6 4.3 %fusion.4.refs_0_ = f32[352,1024]{1,0:T(8,128)} fusion(bf16[4096,2048]{1,0:T(8,128)(2,1)S(1)} %copy-done.21, bf16[176,4096]{1,0:T(8,128)(2,1)S(1)} %get-tuple-element.98, bf16[176,4096]{1,0:T(8,128)(2,1)S(1)} %get-tuple-element.97), kind=kOutput, calls=%fused_computation.4 | convolution fusion | flops 2958557184 | bytes 12713984 | tf_op jit(solution)/shard_map/dot_general | solution.py:35
  282.9 4.1 %all-to-all-start.4 = ((f32[16,184,128]{2,1,0:T(8,128)}), f32[16,184,128]{2,1,0:T(8,128)S(1)}, u32[]{:S(2)}, u32[]{:S(2)}) async-start(f32[16,184,128]{2,1,0:T(8,128)} %pack_pairs.3), calls=%async_computation.4 | async-start | bytes 3014656 | tf_op jit(solution)/shard_map/all_to_all | solution.py:43
  287.0 6.3 %fusion.8 = f32[176,1024]{1,0:T(8,128)} fusion(bf16[176,4096]{1,0:T(8,128)(2,1)} %get-tuple-element.72, bf16[4096,2048]{1,0:T(8,128)(2,1)} %all-gather.6.cloned.1.call-done), kind=kOutput, calls=%fused_computation.8 | convolution fusion | flops 1476395008 | bytes 10551296 | tf_op jit(solution)/shard_map/dot_general | solution.py:35
  295.6 3.0 fusion.98
  301.9 3.9 %split_heads.1 = (f32[64,16,64]{2,1,0:T(8,128)}, f32[64,16,64]{2,1,0:T(8,128)}, f32[64,16,64]{2,1,0:T(8,128)}) custom-call(f32[16,96,128]{2,1,0:T(8,128)} %copy-done.3), custom_call_target="tpu_custom_call" | custom-call | tf_op jit(solution)/shard_map/split_heads/pallas_call | solution.py:449
  305.8 6.0 %collective-permute-done.1 = f32[64,1024]{1,0:T(8,128)S(1)} collective-permute-done((f32[64,1024]{1,0:T(8,128)S(1)}, f32[64,1024]{1,0:T(8,128)S(1)}, u32[]{:S(2)}, u32[]{:S(2)}) %collective-permute-start.1) | collective-permute-done | bytes 262176 | tf_op jit(solution)/shard_map/ppermute | solution.py:604
  313.8 3.3 %join_columns.1 = (f32[64,2816]{1,0:T(8,128)}, f32[64,2816]{1,0:T(8,128)}) custom-call(f32[16,184,128]{2,1,0:T(8,128)} %copy-done), custom_call_target="tpu_custom_call" | custom-call | tf_op jit(solution)/shard_map/join_columns/pallas_call | solution.py:434
  (126 shorter events, 54.1 us)
Async XLA Ops:
  7.2 116.2 %all-gather.4.cloned.1.call-start = ((), (), s32[]{:S(2)}) async-start(), calls=%async_computation.5 | async-start | bytes 21168128 | tf_op jit(solution)/shard_map/all_gather | solution.py:39
  91.0 28.1 %copy-start.7 = (bf16[64,4096]{1,0:T(8,128)(2,1)S(1)}, bf16[64,4096]{1,0:T(8,128)(2,1)}, u32[]{:S(2)}) copy-start(bf16[64,4096]{1,0:T(8,128)(2,1)} %slice.182.refs_2_) | copy-start | bytes 1572868
  114.5 14.7 %all-to-all-start = ((bf16[16,64,256]{2,1,0:T(8,128)(2,1)}), bf16[16,64,256]{2,1,0:T(8,128)(2,1)S(1)}, u32[]{:S(2)}, u32[]{:S(2)}) async-start(bf16[16,64,256]{2,1,0:T(8,128)(2,1)} %get-tuple-element.78), calls=%async_computation | async-start | bytes 1048576 | tf_op jit(solution)/shard_map/all_to_all | solution.py:43
  118.7 139.6 %all-gather.6.cloned.1.call-start = ((), (), s32[]{:S(2)}) async-start(), calls=%async_computation.6 | async-start | bytes 17825792 | tf_op jit(solution)/shard_map/all_gather | solution.py:39
  123.4 6.6 %copy-start.5 = (bf16[256,1024]{1,0:T(8,128)(2,1)S(1)}, bf16[256,1024]{1,0:T(8,128)(2,1)}, u32[]{:S(2)}) copy-start(bf16[256,1024]{1,0:T(8,128)(2,1)} %refs_0_.1) | copy-start | bytes 1572868
  128.7 4.9 %copy-start.9 = (bf16[256,1024]{1,0:T(8,128)(2,1)S(1)}, bf16[256,1024]{1,0:T(8,128)(2,1)}, u32[]{:S(2)}) copy-start(bf16[256,1024]{1,0:T(8,128)(2,1)} %param.14) | copy-start | bytes 1572868
  134.7 6.4 %slice-start = ((s8[5767168]{0:T(1024)(128)(4,1)}), s8[1572864]{0:T(1024)(128)(4,1)S(1)}, s32[]{:S(2)}) async-start(s8[5767168]{0:T(1024)(128)(4,1)} %bitcast.55), calls=%async_computation.8 | async-start | bytes 3145728
  134.7 6.3 %slice-start.1 = ((s8[5767168]{0:T(1024)(128)(4,1)}), s8[4194304]{0:T(1024)(128)(4,1)S(1)}, s32[]{:S(2)}) async-start(s8[5767168]{0:T(1024)(128)(4,1)} %bitcast.55), calls=%async_computation.9 | async-start | bytes 8388608
  143.6 7.7 %copy-start.10 = (bf16[256,1024]{1,0:T(8,128)(2,1)S(1)}, bf16[256,1024]{1,0:T(8,128)(2,1)}, u32[]{:S(2)}) copy-start(bf16[256,1024]{1,0:T(8,128)(2,1)} %param.14) | copy-start | bytes 1572868
  151.7 6.9 %copy-start.1 = (bf16[256,1024]{1,0:T(8,128)(2,1)}, bf16[256,1024]{1,0:T(8,128)(2,1)S(1)}, u32[]{:S(2)}) copy-start(bf16[256,1024]{1,0:T(8,128)(2,1)S(1)} %fusion.56) | copy-start | bytes 1572868
  155.0 19.6 %all-to-all-start.1 = ((bf16[16,64,256]{2,1,0:T(8,128)(2,1)}), bf16[16,64,256]{2,1,0:T(8,128)(2,1)S(1)}, u32[]{:S(2)}, u32[]{:S(2)}) async-start(bf16[16,64,256]{2,1,0:T(8,128)(2,1)} %bitcast.11), calls=%async_computation.1 | async-start | bytes 1048576 | tf_op jit(solution)/shard_map/all_to_all | solution.py:43
  158.0 135.3 %all-gather.8.cloned.1.call-start = ((), (), s32[]{:S(2)}) async-start(), calls=%async_computation.7 | async-start | bytes 4718592 | tf_op jit(solution)/shard_map/all_gather | solution.py:572
  222.0 27.2 %all-to-all-start.2 = ((bf16[16,192,256]{2,1,0:T(8,128)(2,1)}), bf16[16,192,256]{2,1,0:T(8,128)(2,1)S(1)}, u32[]{:S(2)}, u32[]{:S(2)}) async-start(bf16[16,192,256]{2,1,0:T(8,128)(2,1)} %get-tuple-element.62), calls=%async_computation.2 | async-start | bytes 3145728 | tf_op jit(solution)/shard_map/all_to_all | solution.py:43
  225.7 67.6 %collective-permute-start = (bf16[8,64,256]{2,1,0:T(8,128)(2,1)S(1)}, bf16[8,64,256]{2,1,0:T(8,128)(2,1)}, u32[]{:S(2)}, u32[]{:S(2)}) collective-permute-start(bf16[8,64,256]{2,1,0:T(8,128)(2,1)S(1)} %constant_dynamic-slice_fusion.1), channel_id=1, source_target_pairs={{0,8},{1,9},{2,10},{3,11},{4,12},{5,13},{6,14},{7,15},{8,0},{9,1},... | collective-permute-start | bytes 786440 | tf_op jit(solution)/shard_map/ppermute | solution.py:570
  253.2 5.1 %copy-start.17 = (bf16[1024,176]{1,0:T(8,128)(2,1)S(1)}, bf16[1024,176]{1,0:T(8,128)(2,1)}, u32[]{:S(2)}) copy-start(bf16[1024,176]{1,0:T(8,128)(2,1)} %get-tuple-element.95) | copy-start | bytes 1081348
  253.2 5.1 %copy-start.18 = (bf16[1024,176]{1,0:T(8,128)(2,1)S(1)}, bf16[1024,176]{1,0:T(8,128)(2,1)}, u32[]{:S(2)}) copy-start(bf16[1024,176]{1,0:T(8,128)(2,1)} %get-tuple-element.96) | copy-start | bytes 1081348
  255.0 27.8 %all-to-all-start.3 = ((f32[16,96,128]{2,1,0:T(8,128)}), f32[16,96,128]{2,1,0:T(8,128)S(1)}, u32[]{:S(2)}, u32[]{:S(2)}) async-start(f32[16,96,128]{2,1,0:T(8,128)} %pack_pairs.2), calls=%async_computation.3 | async-start | bytes 1572864 | tf_op jit(solution)/shard_map/all_to_all | solution.py:43
  258.3 10.5 %copy-start.19 = (bf16[176,1024]{1,0:T(8,128)(2,1)S(1)}, bf16[176,1024]{1,0:T(8,128)(2,1)}, u32[]{:S(2)}) copy-start(bf16[176,1024]{1,0:T(8,128)(2,1)} %down.1) | copy-start | bytes 1081348
  258.3 10.5 %copy-start.21 = (bf16[4096,2048]{1,0:T(8,128)(2,1)S(1)}, bf16[4096,2048]{1,0:T(8,128)(2,1)}, u32[]{:S(2)}) copy-start(bf16[4096,2048]{1,0:T(8,128)(2,1)} %all-gather.6.cloned.1.call-done) | copy-start | bytes 50331652
  282.9 10.5 %copy-start.3 = (f32[16,96,128]{2,1,0:T(8,128)}, f32[16,96,128]{2,1,0:T(8,128)S(1)}, u32[]{:S(2)}) copy-start(f32[16,96,128]{2,1,0:T(8,128)S(1)} %all-to-all-done.3.refs_0_) | copy-start | bytes 2359300
  282.9 29.7 %all-to-all-start.4 = ((f32[16,184,128]{2,1,0:T(8,128)}), f32[16,184,128]{2,1,0:T(8,128)S(1)}, u32[]{:S(2)}, u32[]{:S(2)}) async-start(f32[16,184,128]{2,1,0:T(8,128)} %pack_pairs.3), calls=%async_computation.4 | async-start | bytes 3014656 | tf_op jit(solution)/shard_map/all_to_all | solution.py:43
  295.6 5.1 %copy-start.2 = (bf16[256,1024]{1,0:T(8,128)(2,1)S(1)}, bf16[256,1024]{1,0:T(8,128)(2,1)}, u32[]{:S(2)}) copy-start(bf16[256,1024]{1,0:T(8,128)(2,1)} %copy-done.1) | copy-start | bytes 1572868
  295.6 5.1 %copy-start.15 = (bf16[256,1024]{1,0:T(8,128)(2,1)S(1)}, bf16[256,1024]{1,0:T(8,128)(2,1)}, u32[]{:S(2)}) copy-start(bf16[256,1024]{1,0:T(8,128)(2,1)} %get-tuple-element.122) | copy-start | bytes 1572868
  298.7 13.2 %collective-permute-start.1 = (f32[64,1024]{1,0:T(8,128)S(1)}, f32[64,1024]{1,0:T(8,128)S(1)}, u32[]{:S(2)}, u32[]{:S(2)}) collective-permute-start(f32[64,1024]{1,0:T(8,128)S(1)} %slice.116), channel_id=1, source_target_pairs={{0,8},{1,9},{2,10},{3,11},{4,12},{5,13},{6,14},{7,15},{8,0},{9,1},... | collective-permute-start | bytes 786440 | tf_op jit(solution)/shard_map/ppermute | solution.py:604
  (14 other events, 26.7 us)
Sparse Core Ops, SparseCore 0:
  10.2 113.1 all-gather.3
  134.8 103.7 all-gather.5
  241.1 40.7 all-gather.7
